TPU v7x, 8 devices: a whole 2x2x1 slice. The times are simulated.
8 devices in a mesh: dp: 1 (over z), sp2: 2 (over y), sp: 4 (over x, core).
Axes of the slice: x: 2, y: 2, z: 1, core: 2. Of those that a mesh axis runs over, the one named last changes fastest.
Arguments:
- x: bfloat16 [4, 64, 64, 640], P('dp', 'sp', 'sp2')
- time_emb: bfloat16 [4, 1280], P('dp')
- gn_scale: bfloat16 [5, 640], replicated
- gn_shift: bfloat16 [5, 640], replicated
- conv_w: bfloat16 [4, 3, 3, 640, 640], replicated
- time_w: bfloat16 [2, 1280, 640], replicated
- w_qkv: bfloat16 [3, 640, 8, 80], replicated
- w_out: bfloat16 [8, 80, 640], replicated
Outputs:
- output: bfloat16 [4, 64, 64, 640], P('dp', 'sp', 'sp2')
All inputs are finite; a program needn't handle non-finite values.
Results may differ from a plain program's by a relative error of at most 0.0115244.
Values are sent between devices in bfloat16 or wider.
A program may use at most 1 GiB of HBM per device.

v0:
```python
import jax
import jax.numpy as jnp
from jax import lax
from jax.sharding import PartitionSpec as P

GROUPS = 32
NORM_EPS = 1e-5
SPACE = ("sp", "sp2")


def group_norm(tile, scale, shift, positions):
    batch, tile_rows, tile_cols, channels = tile.shape
    grouped = tile.astype(jnp.float32).reshape(batch, tile_rows, tile_cols, GROUPS, channels // GROUPS)
    local_moments = jnp.stack([jnp.sum(grouped, axis=(1, 2, 4)), jnp.sum(grouped * grouped, axis=(1, 2, 4))])
    moments = lax.psum(local_moments, SPACE)
    count = positions * (channels // GROUPS)
    mean = moments[0] / count
    inv_std = lax.rsqrt(moments[1] / count - mean * mean + NORM_EPS)
    normed = (grouped - mean[:, None, None, :, None]) * inv_std[:, None, None, :, None]
    return normed.reshape(tile.shape) * scale.astype(jnp.float32) + shift.astype(jnp.float32)


def with_halo(tile, row_devs, col_devs):
    down_pairs = [(i, i + 1) for i in range(row_devs - 1)]
    up_pairs = [(i + 1, i) for i in range(row_devs - 1)]
    from_above = lax.ppermute(tile[:, -1:], "sp", down_pairs)
    from_below = lax.ppermute(tile[:, :1], "sp", up_pairs)
    tall = jnp.concatenate([from_above, tile, from_below], axis=1)
    right_pairs = [(j, j + 1) for j in range(col_devs - 1)]
    left_pairs = [(j + 1, j) for j in range(col_devs - 1)]
    from_left = lax.ppermute(tall[:, :, -1:], "sp2", right_pairs)
    from_right = lax.ppermute(tall[:, :, :1], "sp2", left_pairs)
    return jnp.concatenate([from_left, tall, from_right], axis=2)


def conv3x3(padded, kernel):
    return lax.conv_general_dilated(padded, kernel, (1, 1), "VALID", dimension_numbers=("NHWC", "HWIO", "NHWC"), preferred_element_type=jnp.float32)


def res_block(tile, time_vec, gn_scale, gn_shift, conv_w, norm_idx, conv_idx, row_devs, col_devs, positions):
    first = jax.nn.silu(group_norm(tile, gn_scale[norm_idx], gn_shift[norm_idx], positions)).astype(jnp.bfloat16)
    hidden = (conv3x3(with_halo(first, row_devs, col_devs), conv_w[conv_idx]) + time_vec[:, None, None, :]).astype(jnp.bfloat16)
    second = jax.nn.silu(group_norm(hidden, gn_scale[norm_idx + 1], gn_shift[norm_idx + 1], positions)).astype(jnp.bfloat16)
    return (tile.astype(jnp.float32) + conv3x3(with_halo(second, row_devs, col_devs), conv_w[conv_idx + 1])).astype(jnp.bfloat16)


def attention_block(tile, scale, shift, w_qkv, w_out, positions):
    batch, tile_rows, tile_cols, channels = tile.shape
    num_heads, head_dim = w_out.shape[0], w_out.shape[1]
    tokens = tile_rows * tile_cols
    normed = group_norm(tile, scale, shift, positions).astype(jnp.bfloat16)
    query = jnp.einsum("bijc,chd->bijhd", normed, w_qkv[0], preferred_element_type=jnp.float32).astype(jnp.bfloat16).reshape(batch, tokens, num_heads, head_dim)
    key_val = jnp.einsum("bijc,schd->sbijhd", normed, w_qkv[1:], preferred_element_type=jnp.float32).astype(jnp.bfloat16).reshape(2, batch, tokens, num_heads, head_dim)
    gathered = lax.all_gather(key_val, SPACE)
    logit_scale = head_dim ** -0.5

    def absorb(carry, block):
        peak, weight_sum, running_out = carry
        logits = jnp.einsum("bqhd,bkhd->bhqk", query, block[0], preferred_element_type=jnp.float32) * logit_scale
        new_peak = jnp.maximum(peak, jnp.max(logits, axis=-1))
        rescale = jnp.exp(peak - new_peak)
        weights = jnp.exp(logits - new_peak[..., None])
        weight_sum = weight_sum * rescale + jnp.sum(weights, axis=-1)
        running_out = running_out * rescale[..., None] + jnp.einsum("bhqk,bkhd->bhqd", weights.astype(jnp.bfloat16), block[1], preferred_element_type=jnp.float32)
        return (new_peak, weight_sum, running_out), None

    start_carry = (
        jnp.full((batch, num_heads, tokens), -jnp.inf, jnp.float32),
        jnp.zeros((batch, num_heads, tokens), jnp.float32),
        jnp.zeros((batch, num_heads, tokens, head_dim), jnp.float32),
    )
    final_carry, _ = lax.scan(absorb, start_carry, gathered)
    attended = (final_carry[2] / final_carry[1][..., None]).astype(jnp.bfloat16)
    out = jnp.einsum("bhqd,hdc->bqc", attended, w_out, preferred_element_type=jnp.float32)
    return (tile.astype(jnp.float32) + out.reshape(tile.shape)).astype(jnp.bfloat16)


def solution(mesh):
    row_devs = mesh.shape["sp"]
    col_devs = mesh.shape["sp2"]
    lat_spec = P("dp", "sp", "sp2", None)

    def local(x, time_emb, gn_scale, gn_shift, conv_w, time_w, w_qkv, w_out):
        positions = x.shape[1] * row_devs * x.shape[2] * col_devs
        time_act = jax.nn.silu(time_emb.astype(jnp.float32)).astype(jnp.bfloat16)
        time_vecs = jnp.einsum("bt,stc->sbc", time_act, time_w, preferred_element_type=jnp.float32)
        first = res_block(x, time_vecs[0], gn_scale, gn_shift, conv_w, 0, 0, row_devs, col_devs, positions)
        middle = attention_block(first, gn_scale[2], gn_shift[2], w_qkv, w_out, positions)
        return res_block(middle, time_vecs[1], gn_scale, gn_shift, conv_w, 3, 2, row_devs, col_devs, positions)

    return jax.shard_map(local, mesh=mesh, in_specs=(lat_spec, P("dp", None), P(), P(), P(), P(), P(), P()), out_specs=lat_spec, check_vma=False)
```

profile of v0, /device:TPU:1, one launch (start us, length us, event | category | flops | bytes accessed | tf_op | source)
XLA Modules:
  0.0 1064.5 jit_solution(2452440296478725089)
XLA Ops:
  9.8 23.3 %psum.35 = f32[2,4,32]{2,1,0:T(4,128)S(1)} all-reduce(f32[2,4,32]{2,1,0:T(4,128)S(1)} %pad_maximum_fusion.12), channel_id=1, replica_groups=mesh['dp'=1,'sp2'=2,'sp'=4] {'sp','sp2'}, use_global_device_ids=true, to_apply=%region_4.5 | all-reduce | flops 256 | bytes 2048 | tf_op jit(solution)/shard_map/psum | solution.py:15
  39.2 5.3 collective-permute-start
  69.5 31.1 %fusion.143 = (f32[16,32,5,640]{3,1,2,0:T(8,128)}, f32[16,32,5,640]{3,1,2,0:T(8,128)S(1)}) fusion(f32[16,32,5,640]{3,0,2,1:T(8,128)S(1)} %bitcast.259, bf16[4,3,3,640,640]{4,3,2,1,0:T(8,128)(2,1)} %param.14, bf16[18,4,8,7,640]{4,1,3,2,0:T(4,128)(2,1)S(1)} %fusion.65, pred[32,5]{0,1:T(8,128)(4,1)S(1)} %copy-done.15), kind=kOutput, calls=%fused_computation.213 | convolution fusion | flops 18882560000 | bytes 32194720 | tf_op jit(solution)/shard_map/conv_general_dilated | solution.py:37
  104.9 6.7 copy.98
  112.1 20.7 %psum.36 = f32[2,4,32]{2,1,0:T(4,128)S(1)} all-reduce(f32[2,4,32]{2,1,0:T(4,128)S(1)} %pad_maximum_fusion.13), channel_id=1, replica_groups=mesh['dp'=1,'sp2'=2,'sp'=4] {'sp','sp2'}, use_global_device_ids=true, to_apply=%region_9.10 | all-reduce | flops 256 | bytes 2048 | tf_op jit(solution)/shard_map/psum | solution.py:15
  134.2 9.5 multiply_convert_fusion.1
  176.0 28.0 %broadcast_select_fusion.1 = f32[16,32,5,640]{3,1,2,0:T(8,128)S(1)} fusion(pred[32,5]{0,1:T(8,128)(4,1)S(1)} %copy-done.15, bf16[4,3,3,640,640]{4,3,2,1,0:T(8,128)(2,1)} %param.14, bf16[18,4,8,7,640]{4,1,3,2,0:T(4,128)(2,1)S(1)} %fusion.66), kind=kOutput, calls=%fused_computation.118 | convolution fusion | flops 18876006400 | bytes 19087520 | tf_op jit(solution)/shard_map/conv_general_dilated | solution.py:37
  211.7 22.5 %psum.37 = f32[2,4,32]{2,1,0:T(4,128)S(1)} all-reduce(f32[2,4,32]{2,1,0:T(4,128)S(1)} %pad_maximum_fusion.14), channel_id=1, replica_groups=mesh['dp'=1,'sp2'=2,'sp'=4] {'sp','sp2'}, use_global_device_ids=true, to_apply=%region_14.15 | all-reduce | flops 256 | bytes 2048 | tf_op jit(solution)/shard_map/psum | solution.py:15
  237.3 10.1 convert_bitcast_fusion
  247.5 15.1 %copy.110 = bf16[2,4,16,32,8,80]{5,4,3,2,1,0:T(8,128)(2,1)} copy(bf16[2,4,16,32,8,80]{5,3,4,0,2,1:T(8,128)(2,1)} %convert_bitcast_fusion) | data formatting | bytes 10485760 | tf_op jit(solution)/shard_map/convert_element_type | solution.py:53
  262.6 13.4 %copy.111 = bf16[1,2,4,512,8,80]{3,5,4,2,1,0:T(8,128)(2,1)} copy(bf16[1,2,4,512,8,80]{5,4,3,2,1,0:T(8,128)(2,1)} %bitcast.237) | data formatting | bytes 10485760 | tf_op jit(solution)/shard_map/all_gather;reshape | solution.py:54
  280.8 6.1 copy.113
  286.9 5.8 copy.114
  292.7 178.3 %all-gather.2.cloned.1.call-done = bf16[8,2,4,512,8,80]{3,5,4,2,1,0:T(8,128)(2,1)} async-done(((bf16[1,2,4,512,8,80]{3,5,4,2,1,0:T(8,128)(2,1)}), bf16[8,2,4,512,8,80]{3,5,4,2,1,0:T(8,128)(2,1)}) %all-gather.2.cloned.1.call-update) | async-done | bytes 41943056 | tf_op jit(solution)/shard_map/all_gather | solution.py:54
  471.0 377.3 %while.15 = (s32[]{:T(128)}, f32[4,8,512]{2,1,0:T(8,128)S(1)}, f32[4,8,512]{2,1,0:T(8,128)S(1)}, f32[4,8,512,80]{2,3,1,0:T(8,128)}, bf16[8,2,4,512,8,80]{3,5,4,2...) while((s32[]{:T(128)}, f32[4,8,512]{2,1,0:T(8,128)S(1)}, ...), condition=%wide.region_18.19_spmd.clone, body=%wide.region_15.18_spmd.clone.sunk | while | flops 2755477504 | bytes 120063088 | solution.py:72
  471.0 15.1 %bitcast_reduce_fusion.2 = (f32[4,8,512]{2,1,0:T(8,128)S(1)}, f32[4,8,512,512]{3,2,1,0:T(8,128)}) fusion(bf16[4,512,8,80]{1,3,2,0:T(8,128)(2,1)S(1)} %get-tuple-element.210, bf16[8,2,4,512,8,80]{3,5,4,2,1,0:T(8,128)(2,1)} %get-tuple-element.209, s32[]{:T(128)} %get-tuple-element.196), kind=kOutput, calls=%fused_computation.1.clone.1 | convolution fusion | flops 1358938112 | bytes 38863360 | tf_op jit(solution)/shard_map/while/body/eval_jaxpr/bqhd,bkhd->bhqk/dot_general | solution.py:59
  486.1 13.6 %fusion.154 = f32[4,8,512]{2,1,0:T(8,128)S(1)} fusion(f32[4,8,512,512]{3,2,1,0:T(8,128)} %get-tuple-element.184, f32[4,8,512]{2,1,0:T(8,128)S(1)} %select_maximum_fusion.2), kind=kLoop, calls=%fused_computation.4.clone.1 | loop fusion | flops 25149440 | bytes 33685504 | tf_op jit(solution)/shard_map/while/body/eval_jaxpr/reduce_sum | solution.py:63
  499.8 17.1 %fusion.156 = f32[4,8,512,80]{2,3,1,0:T(8,128)} fusion(f32[4,8,512,80]{2,3,1,0:T(8,128)} %get-tuple-element.199, f32[4,8,512]{2,1,0:T(8,128)S(1)} %get-tuple-element.186, pred[]{:T(512)S(6)} %compare.24, f32[4,8,512,512]{3,2,1,0:T(8,128)} %get-tuple-element.184, f32[4,8,512]{2,1,0:T(8,128)S(1)} %select_maximum_fusion.2, ...), kind=kOutput, calls=%fused_computation.9.clone.1 | convolution fusion | flops 1371275264 | bytes 46793220 | tf_op jit(solution)/shard_map/while/body/eval_jaxpr/bhqk,bkhd->bhqd/dot_general | solution.py:64
  516.9 15.1 %bitcast_reduce_fusion.2 = (f32[4,8,512]{2,1,0:T(8,128)S(1)}, f32[4,8,512,512]{3,2,1,0:T(8,128)}) fusion(bf16[4,512,8,80]{1,3,2,0:T(8,128)(2,1)S(1)} %get-tuple-element.210, bf16[8,2,4,512,8,80]{3,5,4,2,1,0:T(8,128)(2,1)} %get-tuple-element.209, s32[]{:T(128)} %get-tuple-element.196), kind=kOutput, calls=%fused_computation.1.clone.1 | convolution fusion | flops 1358938112 | bytes 38863360 | tf_op jit(solution)/shard_map/while/body/eval_jaxpr/bqhd,bkhd->bhqk/dot_general | solution.py:59
  532.0 13.6 %fusion.154 = f32[4,8,512]{2,1,0:T(8,128)S(1)} fusion(f32[4,8,512,512]{3,2,1,0:T(8,128)} %get-tuple-element.184, f32[4,8,512]{2,1,0:T(8,128)S(1)} %select_maximum_fusion.2), kind=kLoop, calls=%fused_computation.4.clone.1 | loop fusion | flops 25149440 | bytes 33685504 | tf_op jit(solution)/shard_map/while/body/eval_jaxpr/reduce_sum | solution.py:63
  545.6 18.6 %fusion.156 = f32[4,8,512,80]{2,3,1,0:T(8,128)} fusion(f32[4,8,512,80]{2,3,1,0:T(8,128)} %get-tuple-element.199, f32[4,8,512]{2,1,0:T(8,128)S(1)} %get-tuple-element.186, pred[]{:T(512)S(6)} %compare.24, f32[4,8,512,512]{3,2,1,0:T(8,128)} %get-tuple-element.184, f32[4,8,512]{2,1,0:T(8,128)S(1)} %select_maximum_fusion.2, ...), kind=kOutput, calls=%fused_computation.9.clone.1 | convolution fusion | flops 1371275264 | bytes 46793220 | tf_op jit(solution)/shard_map/while/body/eval_jaxpr/bhqk,bkhd->bhqd/dot_general | solution.py:64
  564.2 15.1 %bitcast_reduce_fusion.2 = (f32[4,8,512]{2,1,0:T(8,128)S(1)}, f32[4,8,512,512]{3,2,1,0:T(8,128)}) fusion(bf16[4,512,8,80]{1,3,2,0:T(8,128)(2,1)S(1)} %get-tuple-element.210, bf16[8,2,4,512,8,80]{3,5,4,2,1,0:T(8,128)(2,1)} %get-tuple-element.209, s32[]{:T(128)} %get-tuple-element.196), kind=kOutput, calls=%fused_computation.1.clone.1 | convolution fusion | flops 1358938112 | bytes 38863360 | tf_op jit(solution)/shard_map/while/body/eval_jaxpr/bqhd,bkhd->bhqk/dot_general | solution.py:59
  579.3 13.6 %fusion.154 = f32[4,8,512]{2,1,0:T(8,128)S(1)} fusion(f32[4,8,512,512]{3,2,1,0:T(8,128)} %get-tuple-element.184, f32[4,8,512]{2,1,0:T(8,128)S(1)} %select_maximum_fusion.2), kind=kLoop, calls=%fused_computation.4.clone.1 | loop fusion | flops 25149440 | bytes 33685504 | tf_op jit(solution)/shard_map/while/body/eval_jaxpr/reduce_sum | solution.py:63
  593.0 18.6 %fusion.156 = f32[4,8,512,80]{2,3,1,0:T(8,128)} fusion(f32[4,8,512,80]{2,3,1,0:T(8,128)} %get-tuple-element.199, f32[4,8,512]{2,1,0:T(8,128)S(1)} %get-tuple-element.186, pred[]{:T(512)S(6)} %compare.24, f32[4,8,512,512]{3,2,1,0:T(8,128)} %get-tuple-element.184, f32[4,8,512]{2,1,0:T(8,128)S(1)} %select_maximum_fusion.2, ...), kind=kOutput, calls=%fused_computation.9.clone.1 | convolution fusion | flops 1371275264 | bytes 46793220 | tf_op jit(solution)/shard_map/while/body/eval_jaxpr/bhqk,bkhd->bhqd/dot_general | solution.py:64
  611.6 15.1 %bitcast_reduce_fusion.2 = (f32[4,8,512]{2,1,0:T(8,128)S(1)}, f32[4,8,512,512]{3,2,1,0:T(8,128)}) fusion(bf16[4,512,8,80]{1,3,2,0:T(8,128)(2,1)S(1)} %get-tuple-element.210, bf16[8,2,4,512,8,80]{3,5,4,2,1,0:T(8,128)(2,1)} %get-tuple-element.209, s32[]{:T(128)} %get-tuple-element.196), kind=kOutput, calls=%fused_computation.1.clone.1 | convolution fusion | flops 1358938112 | bytes 38863360 | tf_op jit(solution)/shard_map/while/body/eval_jaxpr/bqhd,bkhd->bhqk/dot_general | solution.py:59
  626.7 13.6 %fusion.154 = f32[4,8,512]{2,1,0:T(8,128)S(1)} fusion(f32[4,8,512,512]{3,2,1,0:T(8,128)} %get-tuple-element.184, f32[4,8,512]{2,1,0:T(8,128)S(1)} %select_maximum_fusion.2), kind=kLoop, calls=%fused_computation.4.clone.1 | loop fusion | flops 25149440 | bytes 33685504 | tf_op jit(solution)/shard_map/while/body/eval_jaxpr/reduce_sum | solution.py:63
  640.3 18.6 %fusion.156 = f32[4,8,512,80]{2,3,1,0:T(8,128)} fusion(f32[4,8,512,80]{2,3,1,0:T(8,128)} %get-tuple-element.199, f32[4,8,512]{2,1,0:T(8,128)S(1)} %get-tuple-element.186, pred[]{:T(512)S(6)} %compare.24, f32[4,8,512,512]{3,2,1,0:T(8,128)} %get-tuple-element.184, f32[4,8,512]{2,1,0:T(8,128)S(1)} %select_maximum_fusion.2, ...), kind=kOutput, calls=%fused_computation.9.clone.1 | convolution fusion | flops 1371275264 | bytes 46793220 | tf_op jit(solution)/shard_map/while/body/eval_jaxpr/bhqk,bkhd->bhqd/dot_general | solution.py:64
  658.9 15.1 %bitcast_reduce_fusion.2 = (f32[4,8,512]{2,1,0:T(8,128)S(1)}, f32[4,8,512,512]{3,2,1,0:T(8,128)}) fusion(bf16[4,512,8,80]{1,3,2,0:T(8,128)(2,1)S(1)} %get-tuple-element.210, bf16[8,2,4,512,8,80]{3,5,4,2,1,0:T(8,128)(2,1)} %get-tuple-element.209, s32[]{:T(128)} %get-tuple-element.196), kind=kOutput, calls=%fused_computation.1.clone.1 | convolution fusion | flops 1358938112 | bytes 38863360 | tf_op jit(solution)/shard_map/while/body/eval_jaxpr/bqhd,bkhd->bhqk/dot_general | solution.py:59
  674.0 13.6 %fusion.154 = f32[4,8,512]{2,1,0:T(8,128)S(1)} fusion(f32[4,8,512,512]{3,2,1,0:T(8,128)} %get-tuple-element.184, f32[4,8,512]{2,1,0:T(8,128)S(1)} %select_maximum_fusion.2), kind=kLoop, calls=%fused_computation.4.clone.1 | loop fusion | flops 25149440 | bytes 33685504 | tf_op jit(solution)/shard_map/while/body/eval_jaxpr/reduce_sum | solution.py:63
  687.7 18.6 %fusion.156 = f32[4,8,512,80]{2,3,1,0:T(8,128)} fusion(f32[4,8,512,80]{2,3,1,0:T(8,128)} %get-tuple-element.199, f32[4,8,512]{2,1,0:T(8,128)S(1)} %get-tuple-element.186, pred[]{:T(512)S(6)} %compare.24, f32[4,8,512,512]{3,2,1,0:T(8,128)} %get-tuple-element.184, f32[4,8,512]{2,1,0:T(8,128)S(1)} %select_maximum_fusion.2, ...), kind=kOutput, calls=%fused_computation.9.clone.1 | convolution fusion | flops 1371275264 | bytes 46793220 | tf_op jit(solution)/shard_map/while/body/eval_jaxpr/bhqk,bkhd->bhqd/dot_general | solution.py:64
  706.3 15.1 %bitcast_reduce_fusion.2 = (f32[4,8,512]{2,1,0:T(8,128)S(1)}, f32[4,8,512,512]{3,2,1,0:T(8,128)}) fusion(bf16[4,512,8,80]{1,3,2,0:T(8,128)(2,1)S(1)} %get-tuple-element.210, bf16[8,2,4,512,8,80]{3,5,4,2,1,0:T(8,128)(2,1)} %get-tuple-element.209, s32[]{:T(128)} %get-tuple-element.196), kind=kOutput, calls=%fused_computation.1.clone.1 | convolution fusion | flops 1358938112 | bytes 38863360 | tf_op jit(solution)/shard_map/while/body/eval_jaxpr/bqhd,bkhd->bhqk/dot_general | solution.py:59
  721.4 13.6 %fusion.154 = f32[4,8,512]{2,1,0:T(8,128)S(1)} fusion(f32[4,8,512,512]{3,2,1,0:T(8,128)} %get-tuple-element.184, f32[4,8,512]{2,1,0:T(8,128)S(1)} %select_maximum_fusion.2), kind=kLoop, calls=%fused_computation.4.clone.1 | loop fusion | flops 25149440 | bytes 33685504 | tf_op jit(solution)/shard_map/while/body/eval_jaxpr/reduce_sum | solution.py:63
  735.0 18.6 %fusion.156 = f32[4,8,512,80]{2,3,1,0:T(8,128)} fusion(f32[4,8,512,80]{2,3,1,0:T(8,128)} %get-tuple-element.199, f32[4,8,512]{2,1,0:T(8,128)S(1)} %get-tuple-element.186, pred[]{:T(512)S(6)} %compare.24, f32[4,8,512,512]{3,2,1,0:T(8,128)} %get-tuple-element.184, f32[4,8,512]{2,1,0:T(8,128)S(1)} %select_maximum_fusion.2, ...), kind=kOutput, calls=%fused_computation.9.clone.1 | convolution fusion | flops 1371275264 | bytes 46793220 | tf_op jit(solution)/shard_map/while/body/eval_jaxpr/bhqk,bkhd->bhqd/dot_general | solution.py:64
  753.6 15.1 %bitcast_reduce_fusion.2 = (f32[4,8,512]{2,1,0:T(8,128)S(1)}, f32[4,8,512,512]{3,2,1,0:T(8,128)}) fusion(bf16[4,512,8,80]{1,3,2,0:T(8,128)(2,1)S(1)} %get-tuple-element.210, bf16[8,2,4,512,8,80]{3,5,4,2,1,0:T(8,128)(2,1)} %get-tuple-element.209, s32[]{:T(128)} %get-tuple-element.196), kind=kOutput, calls=%fused_computation.1.clone.1 | convolution fusion | flops 1358938112 | bytes 38863360 | tf_op jit(solution)/shard_map/while/body/eval_jaxpr/bqhd,bkhd->bhqk/dot_general | solution.py:59
  768.7 13.6 %fusion.154 = f32[4,8,512]{2,1,0:T(8,128)S(1)} fusion(f32[4,8,512,512]{3,2,1,0:T(8,128)} %get-tuple-element.184, f32[4,8,512]{2,1,0:T(8,128)S(1)} %select_maximum_fusion.2), kind=kLoop, calls=%fused_computation.4.clone.1 | loop fusion | flops 25149440 | bytes 33685504 | tf_op jit(solution)/shard_map/while/body/eval_jaxpr/reduce_sum | solution.py:63
  782.4 18.6 %fusion.156 = f32[4,8,512,80]{2,3,1,0:T(8,128)} fusion(f32[4,8,512,80]{2,3,1,0:T(8,128)} %get-tuple-element.199, f32[4,8,512]{2,1,0:T(8,128)S(1)} %get-tuple-element.186, pred[]{:T(512)S(6)} %compare.24, f32[4,8,512,512]{3,2,1,0:T(8,128)} %get-tuple-element.184, f32[4,8,512]{2,1,0:T(8,128)S(1)} %select_maximum_fusion.2, ...), kind=kOutput, calls=%fused_computation.9.clone.1 | convolution fusion | flops 1371275264 | bytes 46793220 | tf_op jit(solution)/shard_map/while/body/eval_jaxpr/bhqk,bkhd->bhqd/dot_general | solution.py:64
  801.0 15.1 %bitcast_reduce_fusion.2 = (f32[4,8,512]{2,1,0:T(8,128)S(1)}, f32[4,8,512,512]{3,2,1,0:T(8,128)}) fusion(bf16[4,512,8,80]{1,3,2,0:T(8,128)(2,1)S(1)} %get-tuple-element.210, bf16[8,2,4,512,8,80]{3,5,4,2,1,0:T(8,128)(2,1)} %get-tuple-element.209, s32[]{:T(128)} %get-tuple-element.196), kind=kOutput, calls=%fused_computation.1.clone.1 | convolution fusion | flops 1358938112 | bytes 38863360 | tf_op jit(solution)/shard_map/while/body/eval_jaxpr/bqhd,bkhd->bhqk/dot_general | solution.py:59
  816.1 13.6 %fusion.154 = f32[4,8,512]{2,1,0:T(8,128)S(1)} fusion(f32[4,8,512,512]{3,2,1,0:T(8,128)} %get-tuple-element.184, f32[4,8,512]{2,1,0:T(8,128)S(1)} %select_maximum_fusion.2), kind=kLoop, calls=%fused_computation.4.clone.1 | loop fusion | flops 25149440 | bytes 33685504 | tf_op jit(solution)/shard_map/while/body/eval_jaxpr/reduce_sum | solution.py:63
  829.7 18.6 %fusion.156 = f32[4,8,512,80]{2,3,1,0:T(8,128)} fusion(f32[4,8,512,80]{2,3,1,0:T(8,128)} %get-tuple-element.199, f32[4,8,512]{2,1,0:T(8,128)S(1)} %get-tuple-element.186, pred[]{:T(512)S(6)} %compare.24, f32[4,8,512,512]{3,2,1,0:T(8,128)} %get-tuple-element.184, f32[4,8,512]{2,1,0:T(8,128)S(1)} %select_maximum_fusion.2, ...), kind=kOutput, calls=%fused_computation.9.clone.1 | convolution fusion | flops 1371275264 | bytes 46793220 | tf_op jit(solution)/shard_map/while/body/eval_jaxpr/bhqk,bkhd->bhqd/dot_general | solution.py:64
  848.3 4.9 fusion.97
  853.3 5.0 convert_reduce_fusion
  858.7 21.5 %psum.38 = f32[2,4,32]{2,1,0:T(4,128)S(1)} all-reduce(f32[2,4,32]{2,1,0:T(4,128)S(1)} %pad_maximum_fusion.15), channel_id=1, replica_groups=mesh['dp'=1,'sp2'=2,'sp'=4] {'sp','sp2'}, use_global_device_ids=true, to_apply=%region_23.24 | all-reduce | flops 256 | bytes 2048 | tf_op jit(solution)/shard_map/psum | solution.py:15
  884.7 5.3 collective-permute-start.8
  916.0 31.0 %fusion.144 = (f32[16,32,5,640]{3,1,2,0:T(8,128)}, f32[16,32,5,640]{3,1,2,0:T(8,128)S(1)}) fusion(f32[16,32,5,640]{3,0,2,1:T(8,128)S(1)} %bitcast.260, bf16[4,3,3,640,640]{4,3,2,1,0:T(8,128)(2,1)} %param.14, bf16[18,4,8,7,640]{4,1,3,2,0:T(4,128)(2,1)S(1)} %fusion.67, pred[32,5]{0,1:T(8,128)(4,1)S(1)} %copy-done.16), kind=kOutput, calls=%fused_computation.214 | convolution fusion | flops 18882560000 | bytes 32194720 | tf_op jit(solution)/shard_map/conv_general_dilated | solution.py:37
  951.3 6.7 copy.120
  958.5 20.9 %psum.39 = f32[2,4,32]{2,1,0:T(4,128)S(1)} all-reduce(f32[2,4,32]{2,1,0:T(4,128)S(1)} %pad_maximum_fusion.16), channel_id=1, replica_groups=mesh['dp'=1,'sp2'=2,'sp'=4] {'sp','sp2'}, use_global_device_ids=true, to_apply=%region_28.29 | all-reduce | flops 256 | bytes 2048 | tf_op jit(solution)/shard_map/psum | solution.py:15
  980.8 9.5 multiply_convert_fusion
  1022.4 28.0 %broadcast_select_fusion = f32[16,32,5,640]{3,1,2,0:T(8,128)S(1)} fusion(pred[32,5]{0,1:T(8,128)(4,1)S(1)} %copy-done.16, bf16[4,3,3,640,640]{4,3,2,1,0:T(8,128)(2,1)} %param.14, bf16[18,4,8,7,640]{4,1,3,2,0:T(4,128)(2,1)S(1)} %fusion.68), kind=kOutput, calls=%fused_computation.117 | convolution fusion | flops 18876006400 | bytes 19087520 | tf_op jit(solution)/shard_map/conv_general_dilated | solution.py:37
  (221 shorter events, 164.3 us)
Async XLA Ops:
  6.5 39.9 %copy-start = (bf16[2,1280,640]{2,1,0:T(8,128)(2,1)S(1)}, bf16[2,1280,640]{2,1,0:T(8,128)(2,1)}, u32[]{:S(2)}) copy-start(bf16[2,1280,640]{2,1,0:T(8,128)(2,1)} %param.15) | copy-start | bytes 9830404
  6.5 39.9 %copy-start.14 = (bf16[4,1280]{1,0:T(4,128)(2,1)S(1)}, bf16[4,1280]{1,0:T(4,128)(2,1)}, u32[]{:S(2)}) copy-start(bf16[4,1280]{1,0:T(4,128)(2,1)} %param.11) | copy-start | bytes 30724
  6.5 464.5 %all-gather.2.cloned.1.call-start = ((), (), s32[]{:S(2)}) async-start(), calls=%async_computation | async-start | bytes 47185920 | tf_op jit(solution)/shard_map/all_gather | solution.py:54
  39.2 9.3 collective-permute-start
  44.5 8.4 collective-permute-start.1
  53.0 4.1 collective-permute-start.2
  55.2 5.6 collective-permute-start.3
  68.8 0.7 copy-start.15
  100.6 3.8 copy-start.3
  147.7 9.9 collective-permute-start.5
  151.2 6.0 collective-permute-start.4
  157.7 5.7 collective-permute-start.6
  161.4 6.2 collective-permute-start.7
  204.0 4.2 copy-start.5
  208.2 26.3 %copy-start.8 = (f32[640]{0:T(1024)S(1)}, f32[640]{0:T(1024)}, u32[]{:S(2)}) copy-start(f32[640]{0:T(1024)} %get-tuple-element.91) | copy-start | bytes 7684
  208.2 26.3 %copy-start.9 = (f32[640]{0:T(1024)S(1)}, f32[640]{0:T(1024)}, u32[]{:S(2)}) copy-start(f32[640]{0:T(1024)} %get-tuple-element.140) | copy-start | bytes 7684
  848.3 4.9 copy-start.6
  853.3 27.3 %copy-start.10 = (f32[640]{0:T(1024)S(1)}, f32[640]{0:T(1024)}, u32[]{:S(2)}) copy-start(f32[640]{0:T(1024)} %get-tuple-element.94) | copy-start | bytes 7684
  853.3 27.3 %copy-start.11 = (f32[640]{0:T(1024)S(1)}, f32[640]{0:T(1024)}, u32[]{:S(2)}) copy-start(f32[640]{0:T(1024)} %get-tuple-element.137) | copy-start | bytes 7684
  884.7 9.3 collective-permute-start.8
  890.0 8.4 collective-permute-start.9
  898.5 5.0 collective-permute-start.10
  901.6 5.6 collective-permute-start.11
  912.9 2.4 copy-start.7
  915.3 0.7 copy-start.16
  946.9 3.8 copy-start.2
  979.8 1.0 copy-start.12
  979.8 1.0 copy-start.13
  994.3 9.9 collective-permute-start.13
  997.8 6.0 collective-permute-start.12
  1004.3 5.7 collective-permute-start.14
  1008.0 6.2 collective-permute-start.15
  1050.4 4.1 copy-start.4
  1054.5 2.8 copy-start.1
Sparse Core Ops, SparseCore 0:
  276.1 194.9 all-gather.1
where the time goes:
time: 1080 us; the launch traced here: 1060 us
  matrix products  406 us (38%)
  waiting for transfers between devices  209 us (19%)
  other arithmetic  174 us (16%)
  blocking collectives  109 us (10%)
  local copies, waits for them, and re-layouts  104 us (10%)
  starting transfers between devices  46.3 us (4%)
  between operations  14.9 us (1%)
    all_gather x1, waiting for transfers between devices, attention_block(): gathered = lax.all_gather(key_val, SPACE)  178 us
    dot_general x8, matrix products, absorb(): jnp.einsum('bhqk,bkhd->bhqd', weights.astype(jnp.bfloat16), block[1], pre...  147 us
    dot_general x8, matrix products, absorb(): jnp.einsum('bqhd,bkhd->bhqk', query, block[0], preferred_element_type=jnp...  121 us
    conv_general_dilated x4, matrix products, conv3x3(): lax.conv_general_dilated(padded, kernel, (1, 1), 'VALID', dimension_numbe...  118 us
    psum x5, blocking collectives, group_norm(): moments = lax.psum(local_moments, SPACE)  109 us
    reduce_sum x8, other arithmetic, absorb(): weight_sum = weight_sum * rescale + jnp.sum(weights, axis=-1)  109 us
  transfers between devices with their start and end apart: 17, of which 16 were waited for; matrix products, arithmetic and copies ran while one was open for 2% of the time, Pallas kernels for 0%

commit v1 on v0

v1 whole, which is shorter than its diff:
```python
import functools

import jax
import jax.numpy as jnp
from jax import lax
from jax.experimental import pallas as pl
from jax.experimental.pallas import tpu as pltpu
from jax.sharding import PartitionSpec as P

GROUPS = 32
NORM_EPS = 1e-5
LANES = 128
CHUNK_ROWS = 4
QUERY_BLOCK = 512
KEY_BLOCK = 512
MESH = pl.DeviceIdType.MESH
F32 = jnp.float32
BF16 = jnp.bfloat16


def position():
    sp = lax.axis_index("sp")
    return lax.div(sp, 2), lax.rem(sp, 2), lax.axis_index("sp2")


def partner_id():
    chip_x, core, _ = position()
    return {"sp": 2 * chip_x + 1 - core}


def barrier_pair():
    sem = pltpu.get_barrier_semaphore()
    pl.semaphore_signal(sem, inc=1, device_id=partner_id(), device_id_type=MESH)
    pl.semaphore_wait(sem, 1)


def barrier_all():
    sem = pltpu.get_barrier_semaphore()
    sp, col = lax.axis_index("sp"), lax.axis_index("sp2")
    for i in range(4):
        for j in range(2):
            if i or j:
                target = {"sp": lax.rem(sp + i, 4), "sp2": lax.rem(col + j, 2)}
                pl.semaphore_signal(sem, inc=1, device_id=target, device_id_type=MESH)
    pl.semaphore_wait(sem, 7)


def split3(value):
    high = value.astype(BF16).astype(F32)
    rest = value - high
    mid = rest.astype(BF16).astype(F32)
    low = rest - mid
    return jnp.concatenate([high, mid, low, jnp.zeros_like(value)], axis=0).astype(BF16)


def exact_dot(value, one_hot):
    out = jnp.dot(split3(value), one_hot, preferred_element_type=F32)
    return out[0:8] + out[8:16] + out[16:24]


def group_matrices(channels):
    width = channels // GROUPS
    chan = lax.broadcasted_iota(jnp.int32, (channels, LANES), 0)
    grp = lax.broadcasted_iota(jnp.int32, (channels, LANES), 1) * width
    gather = jnp.where((chan >= grp) & (chan < grp + width), 1.0, 0.0).astype(BF16)
    chan_t = lax.broadcasted_iota(jnp.int32, (LANES, channels), 1)
    grp_t = lax.broadcasted_iota(jnp.int32, (LANES, channels), 0) * width
    spread = jnp.where((chan_t >= grp_t) & (chan_t < grp_t + width), 1.0, 0.0).astype(BF16)
    return gather, spread


def norm_params(sums, count):
    gather, spread = group_matrices(sums.shape[1])
    group_sums = exact_dot(sums, gather)
    mean = group_sums[0:1] / count
    inv_std = lax.rsqrt(group_sums[1:2] / count - mean * mean + NORM_EPS)
    stacked = jnp.concatenate([mean, inv_std, jnp.zeros((6, LANES), F32)], axis=0)
    per_channel = exact_dot(stacked, spread)
    return per_channel[0:1], per_channel[1:2]


def fold_rows(value):
    rows, channels = value.shape
    return jnp.sum(value.reshape(rows // 8, 8, channels), axis=0)


def add_moments(acc_ref, value):
    acc_ref[0] += fold_rows(value)
    acc_ref[1] += fold_rows(value * value)


def moment_rows(acc_ref):
    total = jnp.sum(acc_ref[0], axis=0, keepdims=True)
    square = jnp.sum(acc_ref[1], axis=0, keepdims=True)
    return jnp.concatenate([total, square, jnp.zeros((6, total.shape[1]), F32)], axis=0)


def exchange(slot, send_ref, recv_ref, send_sem, recv_sem):
    copy = pltpu.make_async_remote_copy(
        src_ref=send_ref.at[slot],
        dst_ref=recv_ref.at[slot],
        send_sem=send_sem.at[slot],
        recv_sem=recv_sem.at[slot],
        device_id=partner_id(),
        device_id_type=MESH,
    )
    copy.start()
    copy.wait()
    return send_ref[slot] + recv_ref[slot]


def silu(value):
    half = 0.5 * value
    return half + half * jnp.tanh(half)


def res_kernel(norm_idx, conv_idx, count, first, *refs):
    if first:
        (x_ref, time_ref, scale_ref, shift_ref, w_ref, out_ref, stat_ref,
         a_ref, u_ref, h_ref, w_vmem, acc_ref, st_send, st_recv,
         w_sem, st_ssem, st_rsem, halo_ssem, halo_rsem, tile_ssem, tile_rsem) = refs
    else:
        (a_hbm, stat_in, time_ref, scale_ref, shift_ref, w_ref, out_ref,
         a_ref, u_ref, h_ref, w_vmem, acc_ref, st_send, st_recv,
         w_sem, st_ssem, st_rsem, halo_ssem, halo_rsem, tile_ssem, tile_rsem, a_sem) = refs
    rows, cols, channels = a_ref.shape
    tile_rows, tile_cols = rows // 2, cols // 2
    chip_x, core, chip_y = position()
    sp = lax.axis_index("sp")

    weights = [pltpu.make_async_copy(w_ref.at[conv_idx + k], w_vmem.at[k], w_sem.at[k]) for k in range(2)]
    for copy in weights:
        copy.start()
    if not first:
        a_copy = pltpu.make_async_copy(a_hbm, a_ref, a_sem)
        a_copy.start()
    barrier_all()

    def tile_of(ref, part_row, part_col):
        return ref.at[pl.ds(part_row * tile_rows, tile_rows), pl.ds(part_col * tile_cols, tile_cols)]

    if first:
        slot = 2 * chip_y + core
        for k in (3, 2, 1, 0):
            to_x, to_y = lax.rem(chip_x + k // 2, 2), lax.rem(chip_y + k % 2, 2)
            to_sp = 2 * to_x + chip_x
            here = (to_sp == sp) & (to_y == chip_y)
            src = x_ref.at[2 * to_x + to_y]
            dst = tile_of(a_ref, core, chip_y)
            remote = pltpu.make_async_remote_copy(
                src_ref=src, dst_ref=dst, send_sem=tile_ssem.at[k], recv_sem=tile_rsem.at[slot],
                device_id={"sp": to_sp, "sp2": to_y}, device_id_type=MESH)
            if k:
                remote.start()
            else:
                @pl.when(here)
                def _():
                    pltpu.make_async_copy(src, dst, tile_rsem.at[slot]).start()

                @pl.when(jnp.logical_not(here))
                def _():
                    remote.start()
        acc_ref[...] = jnp.zeros_like(acc_ref)
        for part in range(4):
            landed = tile_of(a_ref, part % 2, part // 2)
            pltpu.make_async_copy(landed, landed, tile_rsem.at[part]).wait()

        def add_row(row, carry):
            add_moments(acc_ref, a_ref[row].astype(F32))
            return carry

        lax.fori_loop(0, rows, add_row, 0)
        st_send[0] = moment_rows(acc_ref)
    else:
        st_send[0] = stat_in[...]
        a_copy.wait()

    def fill(src_ref, mean, gain, shift):
        place = lax.broadcasted_iota(jnp.int32, (cols, channels), 0)

        def fill_row(i, carry):
            row = core * i + (1 - core) * (rows - 1 - i)
            value = silu((src_ref[row].astype(F32) - mean) * gain + shift)
            before = jnp.where(place == 0, 0.0, pltpu.roll(value, 1, 0))
            after = jnp.where(place == cols - 1, 0.0, pltpu.roll(value, cols - 1, 0))
            u_ref[row + 1, :, 0:channels] = before.astype(BF16)
            u_ref[row + 1, :, channels:2 * channels] = value.astype(BF16)
            u_ref[row + 1, :, 2 * channels:3 * channels] = after.astype(BF16)
            return carry

        lax.fori_loop(0, 4, fill_row, 0)
        return fill_row

    for k in range(2):
        src_ref = a_ref if k == 0 else h_ref
        sums = exchange(k, st_send, st_recv, st_ssem, st_rsem)
        mean, inv_std = norm_params(sums, count)
        gain = inv_std * scale_ref[norm_idx + k:norm_idx + k + 1].astype(F32)
        shift = shift_ref[norm_idx + k:norm_idx + k + 1].astype(F32)
        fill_row = fill(src_ref, mean, gain, shift)
        halo = pltpu.make_async_remote_copy(
            src_ref=u_ref.at[rows - (rows - 1) * core],
            dst_ref=u_ref.at[(rows + 1) * core],
            send_sem=halo_ssem.at[k],
            recv_sem=halo_rsem.at[k],
            device_id=partner_id(),
            device_id_type=MESH,
        )
        if k == 0:
            u_ref[(rows + 1) * core] = jnp.zeros((cols, 3 * channels), BF16)
        halo.start()
        lax.fori_loop(4, rows, fill_row, 0)
        weights[k].wait()
        acc_ref[...] = jnp.zeros_like(acc_ref)
        halo.wait()

        def conv_chunk(i, carry):
            chunk = i * CHUNK_ROWS
            total = None
            for dy in range(3):
                lhs = u_ref[pl.ds(chunk + dy, CHUNK_ROWS)].reshape(CHUNK_ROWS * cols, 3 * channels)
                term = jnp.dot(lhs, w_vmem[k, dy], preferred_element_type=F32)
                total = term if total is None else total + term
            if k == 0:
                hidden = (total + time_ref[0:1]).astype(BF16)
                h_ref[pl.ds(chunk, CHUNK_ROWS)] = hidden.reshape(CHUNK_ROWS, cols, channels)
                add_moments(acc_ref, hidden.astype(F32))
            else:
                old = a_ref[pl.ds(chunk, CHUNK_ROWS)].reshape(CHUNK_ROWS * cols, channels)
                new = (old.astype(F32) + total).astype(BF16)
                if first:
                    out_ref[pl.ds(chunk, CHUNK_ROWS)] = new.reshape(CHUNK_ROWS, cols, channels)
                    add_moments(acc_ref, new.astype(F32))
                else:
                    h_ref[pl.ds(chunk, CHUNK_ROWS)] = new.reshape(CHUNK_ROWS, cols, channels)
            return carry

        lax.fori_loop(0, rows // CHUNK_ROWS, conv_chunk, 0)
        if k == 0:
            st_send[1] = moment_rows(acc_ref)

    if first:
        stat_ref[...] = moment_rows(acc_ref)
        for k in range(1, 4):
            pltpu.make_async_remote_copy(
                src_ref=x_ref.at[0], dst_ref=tile_of(a_ref, 0, 0), send_sem=tile_ssem.at[k],
                recv_sem=tile_rsem.at[0], device_id=partner_id(), device_id_type=MESH).wait_send()

        @pl.when(core != chip_x)
        def _():
            pltpu.make_async_remote_copy(
                src_ref=x_ref.at[0], dst_ref=tile_of(a_ref, 0, 0), send_sem=tile_ssem.at[0],
                recv_sem=tile_rsem.at[0], device_id=partner_id(), device_id_type=MESH).wait_send()
    else:
        image = 2 * chip_x + chip_y
        copies = []
        for part in range(4):
            part_row, part_col = part % 2, part // 2
            to_sp = 2 * core + part_row
            here = (to_sp == sp) & (chip_y == part_col)
            src = tile_of(h_ref, part_row, part_col)
            remote = pltpu.make_async_remote_copy(
                src_ref=src, dst_ref=out_ref.at[image], send_sem=tile_ssem.at[part], recv_sem=tile_rsem.at[image],
                device_id={"sp": to_sp, "sp2": part_col}, device_id_type=MESH)
            local = pltpu.make_async_copy(src, out_ref.at[image], tile_rsem.at[image])
            pl.when(here)(local.start)
            pl.when(jnp.logical_not(here))(remote.start)
            copies.append((here, remote))
        for here, remote in copies:
            pl.when(jnp.logical_not(here))(remote.wait_send)
        for slot in range(4):
            pltpu.make_async_copy(out_ref.at[slot], out_ref.at[slot], tile_rsem.at[slot]).wait()


def attention_kernel(norm_idx, count, logit_scale, a_hbm, stat_in, scale_ref, shift_ref, w_hbm, wo_hbm,
                     out_ref, stat_ref, a_ref, n_ref, q_ref, k_ref, v_ref, s_ref, o_ref, w_ref, wo_ref, acc_ref,
                     st_send, st_recv, load_sem, st_ssem, st_rsem, kv_ssem, kv_rsem):
    tokens, channels = a_ref.shape
    heads = q_ref.shape[0]
    step = 256
    loads = [pltpu.make_async_copy(src, dst, load_sem.at[i])
             for i, (src, dst) in enumerate(((a_hbm, a_ref), (w_hbm, w_ref), (wo_hbm, wo_ref)))]
    for load in loads:
        load.start()
    st_send[0] = stat_in[...]
    barrier_pair()
    sums = exchange(0, st_send, st_recv, st_ssem, st_rsem)
    mean, inv_std = norm_params(sums, count)
    gain = inv_std * scale_ref[norm_idx:norm_idx + 1].astype(F32)
    shift = shift_ref[norm_idx:norm_idx + 1].astype(F32)
    loads[0].wait()
    loads[1].wait()

    def kv_copy(which, chunk):
        ref = (k_ref, v_ref)[which]
        return pltpu.make_async_remote_copy(
            src_ref=ref.at[:, pl.ds(chunk * step, step)],
            dst_ref=ref.at[:, pl.ds(tokens + chunk * step, step)],
            send_sem=kv_ssem.at[which, chunk],
            recv_sem=kv_rsem.at[which, chunk],
            device_id=partner_id(),
            device_id_type=MESH,
        )

    chunks = tokens // step

    def key_values(i, carry):
        here = pl.ds(i * step, step)
        normed = ((a_ref[here].astype(F32) - mean) * gain + shift).astype(BF16)
        n_ref[here] = normed
        for which, ref in ((1, k_ref), (2, v_ref)):
            part = jnp.dot(normed, w_ref[which], preferred_element_type=F32).astype(BF16)
            for head in range(heads):
                ref[head, here] = part[:, head * LANES:(head + 1) * LANES]

        @pl.when(i > 0)
        def _():
            kv_copy(0, i - 1).start()
            kv_copy(1, i - 1).start()
        return carry

    lax.fori_loop(0, chunks, key_values, 0)

    def queries(i, carry):
        here = pl.ds(i * step, step)
        part = jnp.dot(n_ref[here], w_ref[0], preferred_element_type=F32).astype(BF16)
        for head in range(heads):
            q_ref[head, here] = part[:, head * LANES:(head + 1) * LANES]

        @pl.when(i == 0)
        def _():
            kv_copy(0, chunks - 1).start()
            kv_copy(1, chunks - 1).start()
        return carry

    lax.fori_loop(0, chunks, queries, 0)

    def arrived(i, carry):
        kv_copy(0, i).wait()
        kv_copy(1, i).wait()
        return carry

    lax.fori_loop(0, chunks, arrived, 0)

    blocks = tokens // QUERY_BLOCK
    key_blocks = 2 * tokens // KEY_BLOCK

    def attend(i, carry):
        head, block = lax.div(i, blocks), lax.rem(i, blocks)
        here = pl.ds(pl.multiple_of(block * QUERY_BLOCK, QUERY_BLOCK), QUERY_BLOCK)
        query = q_ref[head, here]
        peak = None
        for j in range(key_blocks):
            keys = k_ref[head, j * KEY_BLOCK:(j + 1) * KEY_BLOCK]
            scores = lax.dot_general(query, keys, (((1,), (1,)), ((), ())), preferred_element_type=F32)
            s_ref[:, j * KEY_BLOCK:(j + 1) * KEY_BLOCK] = scores
            for part in range(KEY_BLOCK // LANES):
                piece = scores[:, part * LANES:(part + 1) * LANES]
                peak = piece if peak is None else jnp.maximum(peak, piece)
        peak = jnp.max(peak, axis=1, keepdims=True)
        total, attended = None, None
        for j in range(key_blocks):
            weights = jnp.exp2((s_ref[:, j * KEY_BLOCK:(j + 1) * KEY_BLOCK] - peak) * logit_scale)
            for part in range(KEY_BLOCK // LANES):
                piece = weights[:, part * LANES:(part + 1) * LANES]
                total = piece if total is None else total + piece
            term = jnp.dot(weights.astype(BF16), v_ref[head, j * KEY_BLOCK:(j + 1) * KEY_BLOCK], preferred_element_type=F32)
            attended = term if attended is None else attended + term
        total = jnp.sum(total, axis=1, keepdims=True)
        o_ref[here, pl.ds(pl.multiple_of(head * LANES, LANES), LANES)] = (attended / total).astype(BF16)
        return carry

    lax.fori_loop(0, heads * blocks, attend, 0)
    loads[2].wait()
    acc_ref[...] = jnp.zeros_like(acc_ref)

    def project(i, carry):
        here = pl.ds(i * step, step)
        new = (a_ref[here].astype(F32) + jnp.dot(o_ref[here], wo_ref[...], preferred_element_type=F32)).astype(BF16)
        out_ref[here] = new
        add_moments(acc_ref, new.astype(F32))
        return carry

    lax.fori_loop(0, chunks, project, 0)
    stat_ref[...] = moment_rows(acc_ref)


VMEM_SPEC = pl.BlockSpec(memory_space=pltpu.VMEM)
ANY_SPEC = pl.BlockSpec(memory_space=pl.ANY)


def params(collective_id):
    return pltpu.CompilerParams(collective_id=collective_id, has_side_effects=True, vmem_limit_bytes=60 * 2**20)


def res_call(first, norm_idx, conv_idx, count, rows, cols, channels, tile_shape, data, time_vec, scale, shift, w):
    scratch = [
        pltpu.VMEM((rows, cols, channels), BF16),
        pltpu.VMEM((rows + 2, cols, 3 * channels), BF16),
        pltpu.VMEM((rows, cols, channels), BF16),
        pltpu.VMEM((2, 3, 3 * channels, channels), BF16),
        pltpu.VMEM((2, 8, channels), F32),
        pltpu.VMEM((2, 8, channels), F32),
        pltpu.VMEM((2, 8, channels), F32),
        pltpu.SemaphoreType.DMA((2,)),
        pltpu.SemaphoreType.DMA((2,)),
        pltpu.SemaphoreType.DMA((2,)),
        pltpu.SemaphoreType.DMA((2,)),
        pltpu.SemaphoreType.DMA((2,)),
        pltpu.SemaphoreType.DMA((4,)),
        pltpu.SemaphoreType.DMA((4,)),
    ]
    kernel = functools.partial(res_kernel, norm_idx, conv_idx, count, first)
    if first:
        return pl.pallas_call(
            kernel,
            out_shape=[jax.ShapeDtypeStruct((rows, cols, channels), BF16), jax.ShapeDtypeStruct((8, channels), F32)],
            in_specs=[ANY_SPEC, VMEM_SPEC, VMEM_SPEC, VMEM_SPEC, ANY_SPEC],
            out_specs=[VMEM_SPEC, VMEM_SPEC],
            scratch_shapes=scratch,
            compiler_params=params(0),
            name="res_first",
        )(*data, time_vec, scale, shift, w)
    return pl.pallas_call(
        kernel,
        out_shape=jax.ShapeDtypeStruct(tile_shape, BF16),
        in_specs=[ANY_SPEC, VMEM_SPEC, VMEM_SPEC, VMEM_SPEC, VMEM_SPEC, ANY_SPEC],
        out_specs=ANY_SPEC,
        scratch_shapes=scratch + [pltpu.SemaphoreType.DMA],
        compiler_params=params(2),
        name="res_second",
    )(*data, time_vec, scale, shift, w)


def attention_call(norm_idx, count, head_dim, a, stats, scale, shift, w, wo):
    tokens, channels = a.shape
    heads = wo.shape[0] // LANES
    logit_scale = head_dim ** -0.5 * 1.4426950408889634
    return pl.pallas_call(
        functools.partial(attention_kernel, norm_idx, count, logit_scale),
        out_shape=[jax.ShapeDtypeStruct((tokens, channels), BF16), jax.ShapeDtypeStruct((8, channels), F32)],
        in_specs=[ANY_SPEC, VMEM_SPEC, VMEM_SPEC, VMEM_SPEC, ANY_SPEC, ANY_SPEC],
        out_specs=[VMEM_SPEC, VMEM_SPEC],
        scratch_shapes=[
            pltpu.VMEM((tokens, channels), BF16),
            pltpu.VMEM((tokens, channels), BF16),
            pltpu.VMEM((heads, tokens, LANES), BF16),
            pltpu.VMEM((heads, 2 * tokens, LANES), BF16),
            pltpu.VMEM((heads, 2 * tokens, LANES), BF16),
            pltpu.VMEM((QUERY_BLOCK, 2 * tokens), F32),
            pltpu.VMEM((tokens, heads * LANES), BF16),
            pltpu.VMEM(w.shape, BF16),
            pltpu.VMEM(wo.shape, BF16),
            pltpu.VMEM((2, 8, channels), F32),
            pltpu.VMEM((1, 8, channels), F32),
            pltpu.VMEM((1, 8, channels), F32),
            pltpu.SemaphoreType.DMA((3,)),
            pltpu.SemaphoreType.DMA((1,)),
            pltpu.SemaphoreType.DMA((1,)),
            pltpu.SemaphoreType.DMA((2, tokens // 256)),
            pltpu.SemaphoreType.DMA((2, tokens // 256)),
        ],
        compiler_params=params(1),
        name="attention",
    )(a, stats, scale, shift, w, wo)


def solution(mesh):
    lat_spec = P("dp", "sp", "sp2", None)

    def local(x, time_emb, gn_scale, gn_shift, conv_w, time_w, w_qkv, w_out):
        images, tile_rows, tile_cols, channels = x.shape
        rows, cols = 2 * tile_rows, 2 * tile_cols
        count = 2 * rows * cols * (channels // GROUPS)
        heads, head_dim = w_out.shape[0], w_out.shape[1]
        chip_x, _, chip_y = position()
        image = 2 * chip_x + chip_y
        time_act = jax.nn.silu(time_emb.astype(F32)).astype(BF16)
        time_vecs = jnp.einsum("bt,stc->sbc", time_act, time_w, preferred_element_type=F32)
        time_vec = lax.dynamic_slice_in_dim(time_vecs, image, 1, axis=1)
        w = conv_w.reshape(4, 3, 3 * channels, channels)
        pad = LANES - head_dim
        qkv = jnp.pad(w_qkv, ((0, 0), (0, 0), (0, 0), (0, pad))).reshape(3, channels, heads * LANES)
        wo = jnp.pad(w_out, ((0, 0), (0, pad), (0, 0))).reshape(heads * LANES, channels)
        sizes = (count, rows, cols, channels, x.shape)
        first, stats = res_call(True, 0, 0, *sizes, (x,), time_vec[0], gn_scale, gn_shift, w)
        middle, stats = attention_call(2, count, head_dim, first.reshape(rows * cols, channels), stats, gn_scale, gn_shift, qkv, wo)
        return res_call(False, 3, 2, *sizes, (middle.reshape(rows, cols, channels), stats), time_vec[1], gn_scale, gn_shift, w)

    return jax.shard_map(local, mesh=mesh, in_specs=(lat_spec, P("dp", None), P(), P(), P(), P(), P(), P()), out_specs=lat_spec, check_vma=False)
```

time: 1080 us -> 394 us (0.36); the launches traced: 1060 us -> 393 us
  matrix products: 406 us -> 1.24 us
  Pallas kernels: 0 us -> 373 us
  waiting for transfers between devices: 209 us -> 0 us
  other arithmetic: 174 us -> 0 us
  blocking collectives: 109 us -> 0 us
  local copies, waits for them, and re-layouts: 104 us -> 18.8 us
  starting transfers between devices: 46.3 us -> 0 us
  between operations: 14.9 us -> 0.03 us
    pallas_call x0 -> x3, Pallas kernels: none -> 373 us  [the longest x1 200 us: attention_call(): pl.pallas_call(functools.partial(attention_kernel, norm_idx, count, logit...]
    dot_general x20 -> x1, matrix products: 288 us -> 1.24 us  [local(): jnp.einsum('bt,stc->sbc', time_act, time_w, preferred_element_type=F32)]
    all_gather x1 -> x0, waiting for transfers between devices: 178 us -> none  [attention_block(): gathered = lax.all_gather(key_val, SPACE)]
    reduce_sum x25 -> x0, other arithmetic: 122 us -> none  [the longest x8 109 us: absorb(): weight_sum = weight_sum * rescale + jnp.sum(weights, axis=-1)]
    conv_general_dilated x4 -> x0, matrix products: 118 us -> none  [conv3x3(): lax.conv_general_dilated(padded, kernel, (1, 1), 'VALID', dimension_numbe...]
    psum x5 -> x0, blocking collectives: 109 us -> none  [group_norm(): moments = lax.psum(local_moments, SPACE)]
    ppermute x16 -> x0, starting transfers between devices: 46.3 us -> none  [the longest x4 18.2 us: with_halo(): from_above = lax.ppermute(tile[:, -1:], 'sp', down_pairs)]
    convert_element_type x19 -> x0, local copies, waits for them, and re-layouts: 41.1 us -> none  [the longest x1 15.1 us: attention_block(): jnp.einsum('bijc,schd->sbijhd', normed, w_qkv[1:], preferred_element_type...]
  transfers between devices with their start and end apart: 17 -> 0, of which waited for: 16 -> 0; matrix products, arithmetic and copies ran while one was open for 2% -> 0% of each run, Pallas kernels for 0% -> 0%
where the time goes in v1:
time: 394 us; the launch traced here: 393 us
  Pallas kernels  373 us (95%)
  local copies, waits for them, and re-layouts  18.8 us (5%)
    pallas_call x1, Pallas kernels, attention_call(): pl.pallas_call(functools.partial(attention_kernel, norm_idx, count, logit...  200 us
    pallas_call x1, Pallas kernels, res_call(): pl.pallas_call(kernel, out_shape=jax.ShapeDtypeStruct(tile_shape, BF16),...  87.3 us
    pallas_call x1, Pallas kernels, res_call(): pl.pallas_call(kernel, out_shape=[jax.ShapeDtypeStruct((rows, cols, chann...  86.2 us

profile of v1, /device:TPU:1, one launch (start us, length us, event | category | flops | bytes accessed | tf_op | source)
XLA Modules:
  0.0 393.4 jit_solution(16412348392396959775)
XLA Ops:
  0.0 0.0 copy-start
  0.0 1.9 copy-done
  1.9 1.2 fusion.4
  3.2 0.6 dynamic-slice_bitcast_fusion
  3.8 86.2 %res_first.1 = (bf16[32,64,640]{2,1,0:T(8,128)(2,1)}, f32[8,640]{1,0:T(8,128)}) custom-call(bf16[4,16,32,640]{3,2,1,0:T(8,128)(2,1)} %refs_0_.1, f32[1,640]{1,0:T(1,128)} %get-tuple-element.14.refs_1_, bf16[5,640]{1,0:T(8,128)(2,1)} %refs_3_.3, bf16[5,640]{1,0:T(8,128)(2,1)} %refs_4_.1, bf16[4,3,1920,640]{3,2,1,0:T(8,128)(2,1)} %bitcast.13), custom_call_target="tpu_custom_call" | custom-call | tf_op jit(solution)/shard_map/res_first/pallas_call | solution.py:415
  90.0 4.2 %pad.8 = bf16[3,640,8,128]{1,3,2,0:T(8,128)(2,1)} pad(bf16[3,640,8,80]{1,3,2,0:T(8,128)(2,1)} %param.14, bf16[]{:T(256)} %constant.22.clone.1), padding=0_0x0_0x0_0x0_48 | pad | bytes 6389762 | tf_op jit(solution)/shard_map/jit(_pad)/pad | solution.py:483
  94.1 6.3 %copy.10.w_hbm = bf16[3,640,1024]{2,1,0:T(8,128)(2,1)} copy(bf16[3,640,1024]{1,2,0:T(8,128)(2,1)} %bitcast.15) | data formatting | bytes 7864320 | tf_op jit(solution)/shard_map/reshape | solution.py:483
  100.4 2.3 pad.9
  102.7 199.8 %attention.1 = (bf16[2048,640]{1,0:T(8,128)(2,1)}, f32[8,640]{1,0:T(8,128)}) custom-call(bf16[2048,640]{1,0:T(8,128)(2,1)} %bitcast.18, f32[8,640]{1,0:T(8,128)} %get-tuple-element.10.stat_in, bf16[5,640]{1,0:T(8,128)(2,1)} %refs_3_.3, bf16[5,640]{1,0:T(8,128)(2,1)} %refs_4_.1, bf16[3,640,1024]{2,1,0:T(8,128)(2,1)} %copy.10.w_hbm, bf16[1024,640]{1,0:T(8,128)(2,1)} %bitcast.16), custom_call_target="tpu_custom_call" | custom-call | tf_op jit(solution)/shard_map/attention/pallas_call | solution.py:439
  302.6 87.3 %res_second.1 = bf16[4,16,32,640]{3,2,1,0:T(8,128)(2,1)} custom-call(bf16[32,64,640]{2,1,0:T(8,128)(2,1)} %bitcast.17, f32[8,640]{1,0:T(8,128)} %get-tuple-element.12.refs_1_, f32[1,640]{1,0:T(1,128)} %get-tuple-element.13.refs_2_, bf16[5,640]{1,0:T(8,128)(2,1)} %refs_3_.3, bf16[5,640]{1,0:T(8,128)(2,1)} %refs_4_.1, bf16[4,3,1920,640]{3,2,1,0:T(8,128)(2,1)} %bitcast.14), custom_call_target="tpu_custom_call" | custom-call | tf_op jit(solution)/shard_map/res_second/pallas_call | solution.py:424
  389.9 3.5 copy.12
Async XLA Ops:
  0.0 1.9 copy-start

commit v2 on v1

--- a/solution.py
+++ b/solution.py
@@ -13,6 +13,7 @@
 CHUNK_ROWS = 4
 QUERY_BLOCK = 512
 KEY_BLOCK = 512
+TOKEN_BLOCK = 512
 MESH = pl.DeviceIdType.MESH
 F32 = jnp.float32
 BF16 = jnp.bfloat16
@@ -273,15 +274,21 @@
 
 
 def attention_kernel(norm_idx, count, logit_scale, a_hbm, stat_in, scale_ref, shift_ref, w_hbm, wo_hbm,
-                     out_ref, stat_ref, a_ref, n_ref, q_ref, k_ref, v_ref, s_ref, o_ref, w_ref, wo_ref, acc_ref,
-                     st_send, st_recv, load_sem, st_ssem, st_rsem, kv_ssem, kv_rsem):
+                     out_ref, stat_ref, a_ref, n_ref, q_ref, k_ref, v_ref, s_even, s_odd, peak_ref, o_ref,
+                     wq_ref, wk_ref, wv_ref, wo_ref, acc_ref,
+                     st_send, st_recv, load_sem, head_sem, st_ssem, st_rsem, kv_ssem, kv_rsem):
     tokens, channels = a_ref.shape
-    heads = q_ref.shape[0]
-    step = 256
+    heads, head_dim, _ = v_ref.shape
     loads = [pltpu.make_async_copy(src, dst, load_sem.at[i])
-             for i, (src, dst) in enumerate(((a_hbm, a_ref), (w_hbm, w_ref), (wo_hbm, wo_ref)))]
-    for load in loads:
+             for i, (src, dst) in enumerate(((a_hbm, a_ref), (w_hbm.at[2], wv_ref), (w_hbm.at[0], wq_ref), (wo_hbm, wo_ref)))]
+    head_loads = [pltpu.make_async_copy(w_hbm.at[1, pl.ds(head * head_dim, head_dim)],
+                                        wk_ref.at[pl.ds(head * LANES, head_dim)], head_sem.at[head])
+                  for head in range(heads)]
+    for load in loads[:2] + head_loads + loads[2:]:
         load.start()
+    for head in range(heads):
+        wk_ref[head * LANES + head_dim:(head + 1) * LANES] = jnp.zeros((LANES - head_dim, channels), BF16)
+        q_ref[head, head_dim:] = jnp.zeros((LANES - head_dim, tokens), BF16)
     st_send[0] = stat_in[...]
     barrier_pair()
     sums = exchange(0, st_send, st_recv, st_ssem, st_rsem)
@@ -290,28 +297,37 @@
     shift = shift_ref[norm_idx:norm_idx + 1].astype(F32)
     loads[0].wait()
     loads[1].wait()
+    for load in head_loads:
+        load.wait()
+
+    step = TOKEN_BLOCK
+    chunks = tokens // step
+    transposed = (((1,), (1,)), ((), ()))
 
     def kv_copy(which, chunk):
-        ref = (k_ref, v_ref)[which]
+        if which:
+            ref, axis_index = v_ref, (slice(None), slice(None))
+        else:
+            ref, axis_index = k_ref, (slice(None),)
         return pltpu.make_async_remote_copy(
-            src_ref=ref.at[:, pl.ds(chunk * step, step)],
-            dst_ref=ref.at[:, pl.ds(tokens + chunk * step, step)],
+            src_ref=ref.at[axis_index + (pl.ds(pl.multiple_of(chunk * step, step), step),)],
+            dst_ref=ref.at[axis_index + (pl.ds(pl.multiple_of(tokens + chunk * step, step), step),)],
             send_sem=kv_ssem.at[which, chunk],
             recv_sem=kv_rsem.at[which, chunk],
             device_id=partner_id(),
             device_id_type=MESH,
         )
 
-    chunks = tokens // step
-
     def key_values(i, carry):
-        here = pl.ds(i * step, step)
+        here = pl.ds(pl.multiple_of(i * step, step), step)
         normed = ((a_ref[here].astype(F32) - mean) * gain + shift).astype(BF16)
         n_ref[here] = normed
-        for which, ref in ((1, k_ref), (2, v_ref)):
-            part = jnp.dot(normed, w_ref[which], preferred_element_type=F32).astype(BF16)
-            for head in range(heads):
-                ref[head, here] = part[:, head * LANES:(head + 1) * LANES]
+        part = lax.dot_general(normed, wk_ref[...], transposed, preferred_element_type=F32).astype(BF16)
+        for head in range(heads):
+            k_ref[head, here] = part[:, head * LANES:(head + 1) * LANES]
+        part = lax.dot_general(wv_ref[...], normed, transposed, preferred_element_type=F32).astype(BF16)
+        for head in range(heads):
+            v_ref[head, :, here] = part[head * head_dim:(head + 1) * head_dim]
 
         @pl.when(i > 0)
         def _():
@@ -320,12 +336,13 @@
         return carry
 
     lax.fori_loop(0, chunks, key_values, 0)
+    loads[2].wait()
 
     def queries(i, carry):
-        here = pl.ds(i * step, step)
-        part = jnp.dot(n_ref[here], w_ref[0], preferred_element_type=F32).astype(BF16)
+        here = pl.ds(pl.multiple_of(i * step, step), step)
+        part = lax.dot_general(wq_ref[...], n_ref[here], transposed, preferred_element_type=F32).astype(BF16)
         for head in range(heads):
-            q_ref[head, here] = part[:, head * LANES:(head + 1) * LANES]
+            q_ref[head, 0:head_dim, here] = part[head * head_dim:(head + 1) * head_dim]
 
         @pl.when(i == 0)
         def _():
@@ -345,38 +362,54 @@
     blocks = tokens // QUERY_BLOCK
     key_blocks = 2 * tokens // KEY_BLOCK
 
+    def fold(value, combine):
+        return combine(value.reshape(KEY_BLOCK // 8, 8, QUERY_BLOCK), axis=0)
+
+    def interleaved(i, s_ref, s_next, slot):
+        if i is not None:
+            head = lax.div(i, blocks)
+            here = pl.ds(pl.multiple_of(lax.rem(i, blocks) * QUERY_BLOCK, QUERY_BLOCK), QUERY_BLOCK)
+            peak = jnp.max(peak_ref[slot], axis=0, keepdims=True)
+            after = jnp.minimum(i + 1, heads * blocks - 1)
+        else:
+            after = 0
+        next_head = lax.div(after, blocks)
+        next_here = pl.ds(pl.multiple_of(lax.rem(after, blocks) * QUERY_BLOCK, QUERY_BLOCK), QUERY_BLOCK)
+        query = q_ref[next_head, :, next_here]
+        next_peak, total, attended = None, None, None
+        for j in range(key_blocks):
+            keys = slice(j * KEY_BLOCK, (j + 1) * KEY_BLOCK)
+            scores = jnp.dot(k_ref[next_head, keys], query, preferred_element_type=F32)
+            s_next[keys] = scores
+            piece = fold(scores, jnp.max)
+            next_peak = piece if next_peak is None else jnp.maximum(next_peak, piece)
+            if i is not None:
+                weights = jnp.exp2((s_ref[keys] - peak) * logit_scale)
+                piece = fold(weights, jnp.sum)
+                total = piece if total is None else total + piece
+                term = jnp.dot(v_ref[head, :, keys], weights.astype(BF16), preferred_element_type=F32)
+                attended = term if attended is None else attended + term
+        peak_ref[1 - slot] = next_peak
+        if i is not None:
+            total = jnp.sum(total, axis=0, keepdims=True)
+            rows = pl.ds(pl.multiple_of(head * head_dim, 16), head_dim)
+            o_ref[rows, here] = (attended / total).astype(BF16)
+
+    interleaved(None, None, s_even, 1)
+
     def attend(i, carry):
-        head, block = lax.div(i, blocks), lax.rem(i, blocks)
-        here = pl.ds(pl.multiple_of(block * QUERY_BLOCK, QUERY_BLOCK), QUERY_BLOCK)
-        query = q_ref[head, here]
-        peak = None
-        for j in range(key_blocks):
-            keys = k_ref[head, j * KEY_BLOCK:(j + 1) * KEY_BLOCK]
-            scores = lax.dot_general(query, keys, (((1,), (1,)), ((), ())), preferred_element_type=F32)
-            s_ref[:, j * KEY_BLOCK:(j + 1) * KEY_BLOCK] = scores
-            for part in range(KEY_BLOCK // LANES):
-                piece = scores[:, part * LANES:(part + 1) * LANES]
-                peak = piece if peak is None else jnp.maximum(peak, piece)
-        peak = jnp.max(peak, axis=1, keepdims=True)
-        total, attended = None, None
-        for j in range(key_blocks):
-            weights = jnp.exp2((s_ref[:, j * KEY_BLOCK:(j + 1) * KEY_BLOCK] - peak) * logit_scale)
-            for part in range(KEY_BLOCK // LANES):
-                piece = weights[:, part * LANES:(part + 1) * LANES]
-                total = piece if total is None else total + piece
-            term = jnp.dot(weights.astype(BF16), v_ref[head, j * KEY_BLOCK:(j + 1) * KEY_BLOCK], preferred_element_type=F32)
-            attended = term if attended is None else attended + term
-        total = jnp.sum(total, axis=1, keepdims=True)
-        o_ref[here, pl.ds(pl.multiple_of(head * LANES, LANES), LANES)] = (attended / total).astype(BF16)
+        interleaved(2 * i, s_even, s_odd, 0)
+        interleaved(2 * i + 1, s_odd, s_even, 1)
         return carry
 
-    lax.fori_loop(0, heads * blocks, attend, 0)
-    loads[2].wait()
+    lax.fori_loop(0, heads * blocks // 2, attend, 0)
+    loads[3].wait()
     acc_ref[...] = jnp.zeros_like(acc_ref)
 
     def project(i, carry):
-        here = pl.ds(i * step, step)
-        new = (a_ref[here].astype(F32) + jnp.dot(o_ref[here], wo_ref[...], preferred_element_type=F32)).astype(BF16)
+        here = pl.ds(pl.multiple_of(i * step, step), step)
+        added = lax.dot_general(o_ref[:, here], wo_ref[...], (((0,), (0,)), ((), ())), preferred_element_type=F32)
+        new = (a_ref[here].astype(F32) + added).astype(BF16)
         out_ref[here] = new
         add_moments(acc_ref, new.astype(F32))
         return carry
@@ -432,9 +465,9 @@
     )(*data, time_vec, scale, shift, w)
 
 
-def attention_call(norm_idx, count, head_dim, a, stats, scale, shift, w, wo):
+def attention_call(norm_idx, count, heads, a, stats, scale, shift, w, wo):
     tokens, channels = a.shape
-    heads = wo.shape[0] // LANES
+    head_dim = channels // heads
     logit_scale = head_dim ** -0.5 * 1.4426950408889634
     return pl.pallas_call(
         functools.partial(attention_kernel, norm_idx, count, logit_scale),
@@ -444,21 +477,26 @@
         scratch_shapes=[
             pltpu.VMEM((tokens, channels), BF16),
             pltpu.VMEM((tokens, channels), BF16),
-            pltpu.VMEM((heads, tokens, LANES), BF16),
+            pltpu.VMEM((heads, LANES, tokens), BF16),
             pltpu.VMEM((heads, 2 * tokens, LANES), BF16),
-            pltpu.VMEM((heads, 2 * tokens, LANES), BF16),
-            pltpu.VMEM((QUERY_BLOCK, 2 * tokens), F32),
-            pltpu.VMEM((tokens, heads * LANES), BF16),
-            pltpu.VMEM(w.shape, BF16),
-            pltpu.VMEM(wo.shape, BF16),
+            pltpu.VMEM((heads, head_dim, 2 * tokens), BF16),
+            pltpu.VMEM((2 * tokens, QUERY_BLOCK), F32),
+            pltpu.VMEM((2 * tokens, QUERY_BLOCK), F32),
+            pltpu.VMEM((2, 8, QUERY_BLOCK), F32),
+            pltpu.VMEM((channels, tokens), BF16),
+            pltpu.VMEM((channels, channels), BF16),
+            pltpu.VMEM((heads * LANES, channels), BF16),
+            pltpu.VMEM((channels, channels), BF16),
+            pltpu.VMEM((channels, channels), BF16),
             pltpu.VMEM((2, 8, channels), F32),
             pltpu.VMEM((1, 8, channels), F32),
             pltpu.VMEM((1, 8, channels), F32),
-            pltpu.SemaphoreType.DMA((3,)),
+            pltpu.SemaphoreType.DMA((4,)),
+            pltpu.SemaphoreType.DMA((heads,)),
             pltpu.SemaphoreType.DMA((1,)),
             pltpu.SemaphoreType.DMA((1,)),
-            pltpu.SemaphoreType.DMA((2, tokens // 256)),
-            pltpu.SemaphoreType.DMA((2, tokens // 256)),
+            pltpu.SemaphoreType.DMA((2, tokens // TOKEN_BLOCK)),
+            pltpu.SemaphoreType.DMA((2, tokens // TOKEN_BLOCK)),
         ],
         compiler_params=params(1),
         name="attention",
@@ -472,19 +510,18 @@
         images, tile_rows, tile_cols, channels = x.shape
         rows, cols = 2 * tile_rows, 2 * tile_cols
         count = 2 * rows * cols * (channels // GROUPS)
-        heads, head_dim = w_out.shape[0], w_out.shape[1]
+        heads = w_out.shape[0]
         chip_x, _, chip_y = position()
         image = 2 * chip_x + chip_y
         time_act = jax.nn.silu(time_emb.astype(F32)).astype(BF16)
         time_vecs = jnp.einsum("bt,stc->sbc", time_act, time_w, preferred_element_type=F32)
         time_vec = lax.dynamic_slice_in_dim(time_vecs, image, 1, axis=1)
         w = conv_w.reshape(4, 3, 3 * channels, channels)
-        pad = LANES - head_dim
-        qkv = jnp.pad(w_qkv, ((0, 0), (0, 0), (0, 0), (0, pad))).reshape(3, channels, heads * LANES)
-        wo = jnp.pad(w_out, ((0, 0), (0, pad), (0, 0))).reshape(heads * LANES, channels)
+        qkv = jnp.transpose(w_qkv, (0, 2, 3, 1)).reshape(3, channels, channels)
+        wo = w_out.reshape(channels, channels)
         sizes = (count, rows, cols, channels, x.shape)
         first, stats = res_call(True, 0, 0, *sizes, (x,), time_vec[0], gn_scale, gn_shift, w)
-        middle, stats = attention_call(2, count, head_dim, first.reshape(rows * cols, channels), stats, gn_scale, gn_shift, qkv, wo)
+        middle, stats = attention_call(2, count, heads, first.reshape(rows * cols, channels), stats, gn_scale, gn_shift, qkv, wo)
         return res_call(False, 3, 2, *sizes, (middle.reshape(rows, cols, channels), stats), time_vec[1], gn_scale, gn_shift, w)
 
     return jax.shard_map(local, mesh=mesh, in_specs=(lat_spec, P("dp", None), P(), P(), P(), P(), P(), P()), out_specs=lat_spec, check_vma=False)

time: 394 us -> 269 us (0.68)
  Pallas kernels: 373 us -> 262 us
  local copies, waits for them, and re-layouts: 18.8 us -> 6.05 us
    pallas_call x1, Pallas kernels: 200 us -> 88.2 us  [attention_call(): pl.pallas_call(functools.partial(attention_kernel, norm_idx, count, logit...]
    pad x2 -> x0, local copies, waits for them, and re-layouts: 6.47 us -> none  [the longest x1 4.16 us: local(): jnp.pad(w_qkv, ((0, 0), (0, 0), (0, 0), (0, pad)))]
    reshape x1 -> x0, local copies, waits for them, and re-layouts: 6.28 us -> none  [local(): jnp.pad(w_qkv, ((0, 0), (0, 0), (0, 0), (0, pad)))]
where the time goes in v2:
time: 269 us
  Pallas kernels  262 us (97%)
  local copies, waits for them, and re-layouts  6.05 us (2%)
    pallas_call x1, Pallas kernels, attention_call(): pl.pallas_call(functools.partial(attention_kernel, norm_idx, count, logit...  88.2 us
    pallas_call x1, Pallas kernels, res_call(): pl.pallas_call(kernel, out_shape=jax.ShapeDtypeStruct(tile_shape, BF16),...  87.2 us
    pallas_call x1, Pallas kernels, res_call(): pl.pallas_call(kernel, out_shape=[jax.ShapeDtypeStruct((rows, cols, chann...  86.1 us
    unnamed x3, local copies, waits for them, and re-layouts  5.44 us

profile of v2, /device:TPU:1, one launch (start us, length us, event | category | flops | bytes accessed | tf_op | source)
XLA Modules:
  0.0 268.8 jit_solution(17677489592362732299)
XLA Ops:
  0.0 0.0 copy-start
  0.0 1.9 copy-done
  1.9 1.2 fusion.4
  3.2 0.6 dynamic-slice_bitcast_fusion
  3.8 86.1 %res_first.1 = (bf16[32,64,640]{2,1,0:T(8,128)(2,1)}, f32[8,640]{1,0:T(8,128)}) custom-call(bf16[4,16,32,640]{3,2,1,0:T(8,128)(2,1)} %refs_0_.1, f32[1,640]{1,0:T(1,128)} %get-tuple-element.14.refs_1_, bf16[5,640]{1,0:T(8,128)(2,1)} %refs_3_.3, bf16[5,640]{1,0:T(8,128)(2,1)} %refs_4_.1, bf16[4,3,1920,640]{3,2,1,0:T(8,128)(2,1)} %bitcast.15), custom_call_target="tpu_custom_call" | custom-call | tf_op jit(solution)/shard_map/res_first/pallas_call | solution.py:448
  89.9 88.2 %attention.1 = (bf16[2048,640]{1,0:T(8,128)(2,1)}, f32[8,640]{1,0:T(8,128)}) custom-call(bf16[2048,640]{1,0:T(8,128)(2,1)} %bitcast.18, f32[8,640]{1,0:T(8,128)} %get-tuple-element.10.stat_in, bf16[5,640]{1,0:T(8,128)(2,1)} %refs_3_.3, bf16[5,640]{1,0:T(8,128)(2,1)} %refs_4_.1, bf16[3,640,640]{2,1,0:T(8,128)(2,1)} %bitcast.19, bf16[640,640]{1,0:T(8,128)(2,1)} %bitcast.20), custom_call_target="tpu_custom_call" | custom-call | tf_op jit(solution)/shard_map/attention/pallas_call | solution.py:472
  178.1 87.2 %res_second.1 = bf16[4,16,32,640]{3,2,1,0:T(8,128)(2,1)} custom-call(bf16[32,64,640]{2,1,0:T(8,128)(2,1)} %bitcast.17, f32[8,640]{1,0:T(8,128)} %get-tuple-element.12.refs_1_, f32[1,640]{1,0:T(1,128)} %get-tuple-element.13.refs_2_, bf16[5,640]{1,0:T(8,128)(2,1)} %refs_3_.3, bf16[5,640]{1,0:T(8,128)(2,1)} %refs_4_.1, bf16[4,3,1920,640]{3,2,1,0:T(8,128)(2,1)} %bitcast.16), custom_call_target="tpu_custom_call" | custom-call | tf_op jit(solution)/shard_map/res_second/pallas_call | solution.py:457
  265.3 3.5 %copy.10 = bf16[4,16,32,640]{3,2,1,0:T(8,128)(2,1)} copy(bf16[4,16,32,640]{3,2,1,0:T(8,128)(2,1)} %res_second.1) | data formatting | bytes 5242880
Async XLA Ops:
  0.0 1.9 copy-start

commit v3 on v2

--- a/solution.py
+++ b/solution.py
@@ -11,6 +11,8 @@
 NORM_EPS = 1e-5
 LANES = 128
 CHUNK_ROWS = 4
+CHUNKS = 8
+PIECES = ((0, 5), (5, 4), (9, 4), (13, 3))
 QUERY_BLOCK = 512
 KEY_BLOCK = 512
 TOKEN_BLOCK = 512
@@ -35,15 +37,18 @@
     pl.semaphore_wait(sem, 1)
 
 
-def barrier_all():
-    sem = pltpu.get_barrier_semaphore()
+def others():
     sp, col = lax.axis_index("sp"), lax.axis_index("sp2")
-    for i in range(4):
-        for j in range(2):
-            if i or j:
-                target = {"sp": lax.rem(sp + i, 4), "sp2": lax.rem(col + j, 2)}
-                pl.semaphore_signal(sem, inc=1, device_id=target, device_id_type=MESH)
-    pl.semaphore_wait(sem, 7)
+    return [(lax.rem(sp + i, 4), lax.rem(col + j, 2)) for i in range(4) for j in range(2) if i or j]
+
+
+def signal_all():
+    for sp, col in others():
+        pl.semaphore_signal(pltpu.get_barrier_semaphore(), inc=1, device_id={"sp": sp, "sp2": col}, device_id_type=MESH)
+
+
+def wait_all():
+    pl.semaphore_wait(pltpu.get_barrier_semaphore(), 7)
 
 
 def split3(value):
@@ -70,14 +75,17 @@
     return gather, spread
 
 
-def norm_params(sums, count):
-    gather, spread = group_matrices(sums.shape[1])
-    group_sums = exact_dot(sums, gather)
+def spread_groups(group_sums, spread, count):
     mean = group_sums[0:1] / count
     inv_std = lax.rsqrt(group_sums[1:2] / count - mean * mean + NORM_EPS)
     stacked = jnp.concatenate([mean, inv_std, jnp.zeros((6, LANES), F32)], axis=0)
     per_channel = exact_dot(stacked, spread)
     return per_channel[0:1], per_channel[1:2]
+
+
+def norm_params(sums, count):
+    gather, spread = group_matrices(sums.shape[1])
+    return spread_groups(exact_dot(sums, gather)[0:2], spread, count)
 
 
 def fold_rows(value):
@@ -115,162 +123,323 @@
     return half + half * jnp.tanh(half)
 
 
-def res_kernel(norm_idx, conv_idx, count, first, *refs):
-    if first:
-        (x_ref, time_ref, scale_ref, shift_ref, w_ref, out_ref, stat_ref,
-         a_ref, u_ref, h_ref, w_vmem, acc_ref, st_send, st_recv,
-         w_sem, st_ssem, st_rsem, halo_ssem, halo_rsem, tile_ssem, tile_rsem) = refs
-    else:
-        (a_hbm, stat_in, time_ref, scale_ref, shift_ref, w_ref, out_ref,
-         a_ref, u_ref, h_ref, w_vmem, acc_ref, st_send, st_recv,
-         w_sem, st_ssem, st_rsem, halo_ssem, halo_rsem, tile_ssem, tile_rsem, a_sem) = refs
-    rows, cols, channels = a_ref.shape
+def fill_chunk(u_ref, src_ref, chunk, params, top_edge, bottom_edge):
+    mean, gain, shift = params
+    _, cols, channels = src_ref.shape
+    place = lax.broadcasted_iota(jnp.int32, (cols, channels), 0)
+    last = CHUNK_ROWS + 1
+    for j in range(CHUNK_ROWS + 2):
+        value = silu((src_ref[chunk * CHUNK_ROWS + j].astype(F32) - mean) * gain + shift)
+        if j == 0:
+            value = jnp.where(top_edge & (chunk == 0), 0.0, value)
+        if j == last:
+            value = jnp.where(bottom_edge & (chunk == CHUNKS - 1), 0.0, value)
+        before = jnp.where(place == 0, 0.0, pltpu.roll(value, 1, 0))
+        after = jnp.where(place == cols - 1, 0.0, pltpu.roll(value, cols - 1, 0))
+        u_ref[j, :, 0:channels] = before.astype(BF16)
+        u_ref[j, :, channels:2 * channels] = value.astype(BF16)
+        u_ref[j, :, 2 * channels:3 * channels] = after.astype(BF16)
+
+
+def conv_chunk(u_ref, w):
+    _, cols, depth = u_ref.shape
+    lhs = jnp.concatenate([u_ref[dy:dy + CHUNK_ROWS].reshape(CHUNK_ROWS * cols, depth) for dy in range(3)], axis=1)
+    return jnp.dot(lhs, w[...], preferred_element_type=F32)
+
+
+def conv_loop(order, ready, fill, finish, u_even, u_odd, w):
+    def step(i, half, parity, u_now, u_next):
+        after = jnp.minimum(i + 1, CHUNKS - 1)
+        ready(half, parity)
+        fill(u_next, order(after))
+        finish(order(i), conv_chunk(u_now, w))
+
+    def pair(half, carry):
+        step(2 * half, half, 0, u_even, u_odd)
+        step(2 * half + 1, half, 1, u_odd, u_even)
+        return carry
+
+    fill(u_even, order(jnp.int32(0)))
+    lax.fori_loop(0, CHUNKS // 2, pair, 0)
+
+
+def in_order(i):
+    return i
+
+
+def from_ends(i):
+    return lax.rem(i + 1, 2) * lax.div(i, 2) + lax.rem(i, 2) * (CHUNKS - 1 - lax.div(i, 2))
+
+
+def rows_of(ref, chunk, first=0):
+    value = ref[pl.ds(chunk * CHUNK_ROWS + first, CHUNK_ROWS)]
+    return value.reshape(value.shape[0] * value.shape[1], value.shape[2])
+
+
+def send_edge_row(ref, send_sem, recv_sem, src_ref=None, src_row=None):
+    rows = ref.shape[0] - 2
+    core = position()[1]
+    src = ref.at[rows - (rows - 1) * core] if src_ref is None else src_ref.at[src_row]
+    return pltpu.make_async_remote_copy(
+        src_ref=src, dst_ref=ref.at[(rows + 1) * core],
+        send_sem=send_sem, recv_sem=recv_sem, device_id=partner_id(), device_id_type=MESH)
+
+
+def first_kernel(count, x_ref, emb_ref, scale_ref, shift_ref, w_ref, tw_ref, out_ref, stat_ref, time_ref,
+                 x_vmem, a_ref, h_ref, u_even, u_odd, w_vmem, tw_vmem, acc_ref, time_all, grp_recv, grp_total, st_send, st_recv,
+                 load_sem, grp_ssem, grp_rsem, st_ssem, st_rsem, edge_ssem, edge_rsem, piece_ssem, piece_rsem, halo_ssem, halo_rsem):
+    images, tile_rows, tile_cols, channels = x_ref.shape
+    rows = 2 * tile_rows
+    chip_x, core, chip_y = position()
+    sp = lax.axis_index("sp")
+    me = 2 * sp + chip_y
+    image = 2 * chip_x + chip_y
+
+    signal_all()
+    x_load = pltpu.make_async_copy(x_ref, x_vmem, load_sem.at[0])
+    x_load.start()
+    weights = [pltpu.make_async_copy(w_ref.at[k], w_vmem.at[k], load_sem.at[1 + k]) for k in range(2)]
+    tw_load = pltpu.make_async_copy(tw_ref, tw_vmem, load_sem.at[3])
+    for copy in weights[:1] + [tw_load] + weights[1:]:
+        copy.start()
+
+    gather, spread = group_matrices(channels)
+    x_load.wait()
+    moments = []
+    for i in range(images):
+        acc_ref[...] = jnp.zeros_like(acc_ref)
+
+        def add_row(row, carry):
+            add_moments(acc_ref, x_vmem[i, row].astype(F32))
+            return carry
+
+        lax.fori_loop(0, tile_rows, add_row, 0)
+        moments += [jnp.sum(acc_ref[0], axis=0, keepdims=True), jnp.sum(acc_ref[1], axis=0, keepdims=True)]
+    grp_recv[me] = exact_dot(jnp.concatenate(moments, axis=0), gather)
+    wait_all()
+    group_copies = []
+    for k, (to_sp, to_y) in enumerate(others()):
+        copy = pltpu.make_async_remote_copy(
+            src_ref=grp_recv.at[me], dst_ref=grp_recv.at[me], send_sem=grp_ssem.at[k], recv_sem=grp_rsem.at[me],
+            device_id={"sp": to_sp, "sp2": to_y}, device_id_type=MESH)
+        copy.start()
+        group_copies.append((copy, 2 * to_sp + to_y))
+
+    def piece(part, source_core):
+        low, high = PIECES[part]
+        start = (1 - source_core) * low + source_core * (tile_rows - low - high)
+        return pl.ds(start, high), pl.ds(1 + source_core * tile_rows + start, high)
+
+    def piece_copies(k, part):
+        to_x, to_y = lax.rem(chip_x + k // 2, 2), lax.rem(chip_y + k % 2, 2)
+        src_rows, dst_rows = piece(part, core)
+        src = x_ref.at[2 * to_x + to_y, src_rows]
+        dst = a_ref.at[dst_rows, pl.ds(chip_y * tile_cols, tile_cols)]
+        landed = piece_rsem.at[part, 2 * chip_y + core]
+        remote = pltpu.make_async_remote_copy(
+            src_ref=src, dst_ref=dst, send_sem=piece_ssem.at[k, part], recv_sem=landed,
+            device_id={"sp": 2 * to_x + chip_x, "sp2": to_y}, device_id_type=MESH)
+        return remote, pltpu.make_async_copy(src, dst, landed)
+
+    def halo_copies(k):
+        to_x, to_y = lax.rem(chip_x + k // 2, 2), lax.rem(chip_y + k % 2, 2)
+        src = x_ref.at[2 * to_x + to_y, (tile_rows - 1) * core]
+        dst = a_ref.at[(rows + 1) * chip_x, pl.ds(chip_y * tile_cols, tile_cols)]
+        remote = pltpu.make_async_remote_copy(
+            src_ref=src, dst_ref=dst, send_sem=halo_ssem.at[k], recv_sem=halo_rsem.at[chip_y],
+            device_id={"sp": 2 * to_x + 1 - chip_x, "sp2": to_y}, device_id_type=MESH)
+        return remote, pltpu.make_async_copy(src, dst, halo_rsem.at[chip_y])
+
+    at_home = core == chip_x
+    far_first = (3, 2, 1, 0)
+
+    @pl.when(jnp.logical_not(at_home))
+    def _():
+        for k in far_first:
+            halo_copies(k)[0 if k else 1].start()
+
+    for part in range(len(PIECES)):
+        for k in far_first:
+            remote, local = piece_copies(k, part)
+            if k:
+                remote.start()
+            else:
+                pl.when(at_home)(local.start)
+                pl.when(jnp.logical_not(at_home))(remote.start)
+
+    tw_load.wait()
+    emb = silu(emb_ref[...].astype(F32)).astype(BF16)
+    for k in range(2):
+        time_all[k, 0:images] = jnp.dot(emb, tw_vmem[k], preferred_element_type=F32)
+    time_ref[...] = jnp.broadcast_to(time_all[1, pl.ds(image, 1)], time_ref.shape)
+    time_vec = time_all[0, pl.ds(image, 1)]
+
+    total = jnp.zeros((8, LANES), F32)
+    for copy, _ in group_copies:
+        copy.wait_send()
+    for copy, sender in group_copies:
+        pltpu.make_async_copy(grp_recv.at[sender], grp_recv.at[sender], grp_rsem.at[sender]).wait()
+    for slot in range(8):
+        total = total + grp_recv[slot]
+    grp_total[...] = total
+    mean, inv_std = spread_groups(grp_total[pl.ds(2 * image, 2)], spread, count)
+
+    def wait_piece(part, source_core):
+        for col in range(2):
+            landed = a_ref.at[piece(part, source_core)[1], pl.ds(col * tile_cols, tile_cols)]
+            pltpu.make_async_copy(landed, landed, piece_rsem.at[part, 2 * col + source_core]).wait()
+
+    def ready(half, parity):
+        if parity == 0:
+            for part in range(3):
+                pl.when(half == part)(functools.partial(wait_piece, part, 1))
+        else:
+            for part in range(1, 4):
+                pl.when(half + 1 == part)(functools.partial(wait_piece, part, 0))
+            pl.when(half + 1 == 3)(functools.partial(wait_piece, 3, 1))
+
+    top_edge, bottom_edge = core == 0, core == 1
+
+    def norm(k, mean, inv_std):
+        return mean, inv_std * scale_ref[k:k + 1].astype(F32), shift_ref[k:k + 1].astype(F32)
+
+    params = norm(0, mean, inv_std)
+    for col in range(2):
+        landed = a_ref.at[(rows + 1) * (1 - core), pl.ds(col * tile_cols, tile_cols)]
+        pltpu.make_async_copy(landed, landed, halo_rsem.at[col]).wait()
+    wait_piece(0, 0)
+    acc_ref[...] = jnp.zeros_like(acc_ref)
+    weights[0].wait()
+
+    def finish_first(chunk, total):
+        hidden = (total + time_vec).astype(BF16)
+        h_ref[pl.ds(chunk * CHUNK_ROWS + 1, CHUNK_ROWS)] = hidden.reshape(CHUNK_ROWS, 2 * tile_cols, channels)
+        add_moments(acc_ref, hidden.astype(F32))
+
+    conv_loop(from_ends, ready, lambda u_ref, chunk: fill_chunk(u_ref, a_ref, chunk, params, top_edge, bottom_edge),
+              finish_first, u_even, u_odd, w_vmem.at[0])
+
+    edge = send_edge_row(h_ref, edge_ssem, edge_rsem)
+    edge.start()
+    st_send[0] = moment_rows(acc_ref)
+    acc_ref[...] = jnp.zeros_like(acc_ref)
+    weights[1].wait()
+    second = norm(1, *norm_params(exchange(0, st_send, st_recv, st_ssem, st_rsem), count))
+    edge.wait()
+
+    def finish_second(chunk, total):
+        new = (rows_of(a_ref, chunk, 1).astype(F32) + total).astype(BF16)
+        out_ref[pl.ds(chunk * CHUNK_ROWS, CHUNK_ROWS)] = new.reshape(CHUNK_ROWS, 2 * tile_cols, channels)
+        add_moments(acc_ref, new.astype(F32))
+
+    conv_loop(in_order, lambda half, parity: None,
+              lambda u_ref, chunk: fill_chunk(u_ref, h_ref, chunk, second, top_edge, bottom_edge),
+              finish_second, u_even, u_odd, w_vmem.at[1])
+    stat_ref[...] = moment_rows(acc_ref)
+
+    @pl.when(jnp.logical_not(at_home))
+    def _():
+        for k in (1, 2, 3):
+            halo_copies(k)[0].wait_send()
+
+    for part in range(len(PIECES)):
+        for k in range(4):
+            remote, _ = piece_copies(k, part)
+            if k:
+                remote.wait_send()
+            else:
+                pl.when(jnp.logical_not(at_home))(remote.wait_send)
+
+
+def second_kernel(count, a_hbm, stat_in, time_ref, scale_ref, shift_ref, w_ref, out_ref,
+                  a_ref, h_ref, u_even, u_odd, w_vmem, acc_ref, res_ref, st_send, st_recv,
+                  load_sem, st_ssem, st_rsem, edge_ssem, edge_rsem, tile_ssem, tile_rsem):
+    rows, cols, channels = res_ref.shape
     tile_rows, tile_cols = rows // 2, cols // 2
     chip_x, core, chip_y = position()
     sp = lax.axis_index("sp")
-
-    weights = [pltpu.make_async_copy(w_ref.at[conv_idx + k], w_vmem.at[k], w_sem.at[k]) for k in range(2)]
+    image = 2 * chip_x + chip_y
+
+    signal_all()
+    a_load = pltpu.make_async_copy(a_hbm, a_ref.at[pl.ds(1, rows)], load_sem.at[0])
+    a_load.start()
+    weights = [pltpu.make_async_copy(w_ref.at[2 + k], w_vmem.at[k], load_sem.at[1 + k]) for k in range(2)]
     for copy in weights:
         copy.start()
-    if not first:
-        a_copy = pltpu.make_async_copy(a_hbm, a_ref, a_sem)
-        a_copy.start()
-    barrier_all()
-
-    def tile_of(ref, part_row, part_col):
-        return ref.at[pl.ds(part_row * tile_rows, tile_rows), pl.ds(part_col * tile_cols, tile_cols)]
-
-    if first:
-        slot = 2 * chip_y + core
-        for k in (3, 2, 1, 0):
-            to_x, to_y = lax.rem(chip_x + k // 2, 2), lax.rem(chip_y + k % 2, 2)
-            to_sp = 2 * to_x + chip_x
-            here = (to_sp == sp) & (to_y == chip_y)
-            src = x_ref.at[2 * to_x + to_y]
-            dst = tile_of(a_ref, core, chip_y)
-            remote = pltpu.make_async_remote_copy(
-                src_ref=src, dst_ref=dst, send_sem=tile_ssem.at[k], recv_sem=tile_rsem.at[slot],
-                device_id={"sp": to_sp, "sp2": to_y}, device_id_type=MESH)
-            if k:
-                remote.start()
-            else:
-                @pl.when(here)
-                def _():
-                    pltpu.make_async_copy(src, dst, tile_rsem.at[slot]).start()
-
-                @pl.when(jnp.logical_not(here))
-                def _():
-                    remote.start()
-        acc_ref[...] = jnp.zeros_like(acc_ref)
-        for part in range(4):
-            landed = tile_of(a_ref, part % 2, part // 2)
-            pltpu.make_async_copy(landed, landed, tile_rsem.at[part]).wait()
-
-        def add_row(row, carry):
-            add_moments(acc_ref, a_ref[row].astype(F32))
-            return carry
-
-        lax.fori_loop(0, rows, add_row, 0)
-        st_send[0] = moment_rows(acc_ref)
-    else:
-        st_send[0] = stat_in[...]
-        a_copy.wait()
-
-    def fill(src_ref, mean, gain, shift):
-        place = lax.broadcasted_iota(jnp.int32, (cols, channels), 0)
-
-        def fill_row(i, carry):
-            row = core * i + (1 - core) * (rows - 1 - i)
-            value = silu((src_ref[row].astype(F32) - mean) * gain + shift)
-            before = jnp.where(place == 0, 0.0, pltpu.roll(value, 1, 0))
-            after = jnp.where(place == cols - 1, 0.0, pltpu.roll(value, cols - 1, 0))
-            u_ref[row + 1, :, 0:channels] = before.astype(BF16)
-            u_ref[row + 1, :, channels:2 * channels] = value.astype(BF16)
-            u_ref[row + 1, :, 2 * channels:3 * channels] = after.astype(BF16)
-            return carry
-
-        lax.fori_loop(0, 4, fill_row, 0)
-        return fill_row
-
-    for k in range(2):
-        src_ref = a_ref if k == 0 else h_ref
-        sums = exchange(k, st_send, st_recv, st_ssem, st_rsem)
+    st_send[0] = stat_in[...]
+    acc_ref[...] = jnp.zeros_like(acc_ref)
+    wait_all()
+    edge = send_edge_row(a_ref, edge_ssem.at[0], edge_rsem.at[0], a_hbm, (rows - 1) * (1 - core))
+    edge.start()
+    top_edge, bottom_edge = core == 0, core == 1
+
+    def norm(k, sums):
         mean, inv_std = norm_params(sums, count)
-        gain = inv_std * scale_ref[norm_idx + k:norm_idx + k + 1].astype(F32)
-        shift = shift_ref[norm_idx + k:norm_idx + k + 1].astype(F32)
-        fill_row = fill(src_ref, mean, gain, shift)
-        halo = pltpu.make_async_remote_copy(
-            src_ref=u_ref.at[rows - (rows - 1) * core],
-            dst_ref=u_ref.at[(rows + 1) * core],
-            send_sem=halo_ssem.at[k],
-            recv_sem=halo_rsem.at[k],
-            device_id=partner_id(),
-            device_id_type=MESH,
-        )
-        if k == 0:
-            u_ref[(rows + 1) * core] = jnp.zeros((cols, 3 * channels), BF16)
-        halo.start()
-        lax.fori_loop(4, rows, fill_row, 0)
-        weights[k].wait()
-        acc_ref[...] = jnp.zeros_like(acc_ref)
-        halo.wait()
-
-        def conv_chunk(i, carry):
-            chunk = i * CHUNK_ROWS
-            total = None
-            for dy in range(3):
-                lhs = u_ref[pl.ds(chunk + dy, CHUNK_ROWS)].reshape(CHUNK_ROWS * cols, 3 * channels)
-                term = jnp.dot(lhs, w_vmem[k, dy], preferred_element_type=F32)
-                total = term if total is None else total + term
-            if k == 0:
-                hidden = (total + time_ref[0:1]).astype(BF16)
-                h_ref[pl.ds(chunk, CHUNK_ROWS)] = hidden.reshape(CHUNK_ROWS, cols, channels)
-                add_moments(acc_ref, hidden.astype(F32))
-            else:
-                old = a_ref[pl.ds(chunk, CHUNK_ROWS)].reshape(CHUNK_ROWS * cols, channels)
-                new = (old.astype(F32) + total).astype(BF16)
-                if first:
-                    out_ref[pl.ds(chunk, CHUNK_ROWS)] = new.reshape(CHUNK_ROWS, cols, channels)
-                    add_moments(acc_ref, new.astype(F32))
-                else:
-                    h_ref[pl.ds(chunk, CHUNK_ROWS)] = new.reshape(CHUNK_ROWS, cols, channels)
-            return carry
-
-        lax.fori_loop(0, rows // CHUNK_ROWS, conv_chunk, 0)
-        if k == 0:
-            st_send[1] = moment_rows(acc_ref)
-
-    if first:
-        stat_ref[...] = moment_rows(acc_ref)
-        for k in range(1, 4):
-            pltpu.make_async_remote_copy(
-                src_ref=x_ref.at[0], dst_ref=tile_of(a_ref, 0, 0), send_sem=tile_ssem.at[k],
-                recv_sem=tile_rsem.at[0], device_id=partner_id(), device_id_type=MESH).wait_send()
-
-        @pl.when(core != chip_x)
-        def _():
-            pltpu.make_async_remote_copy(
-                src_ref=x_ref.at[0], dst_ref=tile_of(a_ref, 0, 0), send_sem=tile_ssem.at[0],
-                recv_sem=tile_rsem.at[0], device_id=partner_id(), device_id_type=MESH).wait_send()
-    else:
-        image = 2 * chip_x + chip_y
-        copies = []
-        for part in range(4):
-            part_row, part_col = part % 2, part // 2
-            to_sp = 2 * core + part_row
-            here = (to_sp == sp) & (chip_y == part_col)
-            src = tile_of(h_ref, part_row, part_col)
-            remote = pltpu.make_async_remote_copy(
-                src_ref=src, dst_ref=out_ref.at[image], send_sem=tile_ssem.at[part], recv_sem=tile_rsem.at[image],
-                device_id={"sp": to_sp, "sp2": part_col}, device_id_type=MESH)
-            local = pltpu.make_async_copy(src, out_ref.at[image], tile_rsem.at[image])
+        return mean, inv_std * scale_ref[3 + k:4 + k].astype(F32), shift_ref[3 + k:4 + k].astype(F32)
+
+    params = norm(0, exchange(0, st_send, st_recv, st_ssem, st_rsem))
+    a_load.wait()
+    edge.wait()
+    weights[0].wait()
+    time_vec = time_ref[0:1]
+
+    def finish_first(chunk, total):
+        hidden = (total + time_vec).astype(BF16)
+        h_ref[pl.ds(chunk * CHUNK_ROWS + 1, CHUNK_ROWS)] = hidden.reshape(CHUNK_ROWS, cols, channels)
+        add_moments(acc_ref, hidden.astype(F32))
+
+    conv_loop(in_order, lambda half, parity: None,
+              lambda u_ref, chunk: fill_chunk(u_ref, a_ref, chunk, params, top_edge, bottom_edge),
+              finish_first, u_even, u_odd, w_vmem.at[0])
+
+    edge = send_edge_row(h_ref, edge_ssem.at[1], edge_rsem.at[1])
+    edge.start()
+    st_send[1] = moment_rows(acc_ref)
+    weights[1].wait()
+    second = norm(1, exchange(1, st_send, st_recv, st_ssem, st_rsem))
+    edge.wait()
+
+    per_tile = CHUNKS // 2
+
+    def home_copies(chunk, col):
+        to_sp = 2 * core + lax.div(chunk, per_tile)
+        slot = lax.rem(chunk, per_tile)
+        here = (to_sp == sp) & (chip_y == col)
+        src = res_ref.at[pl.ds(chunk * CHUNK_ROWS, CHUNK_ROWS), pl.ds(col * tile_cols, tile_cols)]
+        dst = out_ref.at[image, pl.ds(slot * CHUNK_ROWS, CHUNK_ROWS)]
+        landed = tile_rsem.at[image, slot]
+        remote = pltpu.make_async_remote_copy(
+            src_ref=src, dst_ref=dst, send_sem=tile_ssem.at[chunk, col], recv_sem=landed,
+            device_id={"sp": to_sp, "sp2": col}, device_id_type=MESH)
+        return here, remote, pltpu.make_async_copy(src, dst, landed)
+
+    def send_home(chunk):
+        for col in range(2):
+            here, remote, local = home_copies(chunk, col)
             pl.when(here)(local.start)
             pl.when(jnp.logical_not(here))(remote.start)
-            copies.append((here, remote))
-        for here, remote in copies:
+
+    def ready(half, parity):
+        if parity:
+            send_home(2 * half)
+        else:
+            pl.when(half > 0)(lambda: send_home(2 * half - 1))
+
+    def finish_second(chunk, total):
+        new = (rows_of(a_ref, chunk, 1).astype(F32) + total).astype(BF16)
+        res_ref[pl.ds(chunk * CHUNK_ROWS, CHUNK_ROWS)] = new.reshape(CHUNK_ROWS, cols, channels)
+
+    conv_loop(in_order, ready, lambda u_ref, chunk: fill_chunk(u_ref, h_ref, chunk, second, top_edge, bottom_edge),
+              finish_second, u_even, u_odd, w_vmem.at[1])
+    send_home(jnp.int32(CHUNKS - 1))
+    for chunk in range(CHUNKS):
+        for col in range(2):
+            here, remote, _ = home_copies(jnp.int32(chunk), col)
             pl.when(jnp.logical_not(here))(remote.wait_send)
-        for slot in range(4):
-            pltpu.make_async_copy(out_ref.at[slot], out_ref.at[slot], tile_rsem.at[slot]).wait()
+    for slot in range(4):
+        for part in range(per_tile):
+            landed = out_ref.at[slot, pl.ds(part * CHUNK_ROWS, CHUNK_ROWS)]
+            pltpu.make_async_copy(landed, landed, tile_rsem.at[slot, part]).wait()
 
 
 def attention_kernel(norm_idx, count, logit_scale, a_hbm, stat_in, scale_ref, shift_ref, w_hbm, wo_hbm,
@@ -426,43 +595,62 @@
     return pltpu.CompilerParams(collective_id=collective_id, has_side_effects=True, vmem_limit_bytes=60 * 2**20)
 
 
-def res_call(first, norm_idx, conv_idx, count, rows, cols, channels, tile_shape, data, time_vec, scale, shift, w):
-    scratch = [
-        pltpu.VMEM((rows, cols, channels), BF16),
-        pltpu.VMEM((rows + 2, cols, 3 * channels), BF16),
-        pltpu.VMEM((rows, cols, channels), BF16),
-        pltpu.VMEM((2, 3, 3 * channels, channels), BF16),
-        pltpu.VMEM((2, 8, channels), F32),
-        pltpu.VMEM((2, 8, channels), F32),
-        pltpu.VMEM((2, 8, channels), F32),
-        pltpu.SemaphoreType.DMA((2,)),
-        pltpu.SemaphoreType.DMA((2,)),
-        pltpu.SemaphoreType.DMA((2,)),
-        pltpu.SemaphoreType.DMA((2,)),
-        pltpu.SemaphoreType.DMA((2,)),
-        pltpu.SemaphoreType.DMA((4,)),
-        pltpu.SemaphoreType.DMA((4,)),
+def conv_scratch(rows, cols, channels):
+    return [
+        pltpu.VMEM((rows + 2, cols, channels), BF16),
+        pltpu.VMEM((rows + 2, cols, channels), BF16),
+        pltpu.VMEM((CHUNK_ROWS + 2, cols, 3 * channels), BF16),
+        pltpu.VMEM((CHUNK_ROWS + 2, cols, 3 * channels), BF16),
+        pltpu.VMEM((2, 9 * channels, channels), BF16),
     ]
-    kernel = functools.partial(res_kernel, norm_idx, conv_idx, count, first)
-    if first:
-        return pl.pallas_call(
-            kernel,
-            out_shape=[jax.ShapeDtypeStruct((rows, cols, channels), BF16), jax.ShapeDtypeStruct((8, channels), F32)],
-            in_specs=[ANY_SPEC, VMEM_SPEC, VMEM_SPEC, VMEM_SPEC, ANY_SPEC],
-            out_specs=[VMEM_SPEC, VMEM_SPEC],
-            scratch_shapes=scratch,
-            compiler_params=params(0),
-            name="res_first",
-        )(*data, time_vec, scale, shift, w)
+
+
+def first_call(count, rows, cols, x, time_emb, scale, shift, w, time_w):
+    channels = x.shape[3]
+    dma = pltpu.SemaphoreType.DMA
     return pl.pallas_call(
-        kernel,
+        functools.partial(first_kernel, count),
+        out_shape=[
+            jax.ShapeDtypeStruct((rows, cols, channels), BF16),
+            jax.ShapeDtypeStruct((8, channels), F32),
+            jax.ShapeDtypeStruct((8, channels), F32),
+        ],
+        in_specs=[ANY_SPEC, VMEM_SPEC, VMEM_SPEC, VMEM_SPEC, ANY_SPEC, ANY_SPEC],
+        out_specs=[VMEM_SPEC, VMEM_SPEC, VMEM_SPEC],
+        scratch_shapes=[pltpu.VMEM(x.shape, BF16)] + conv_scratch(rows, cols, channels) + [
+            pltpu.VMEM(time_w.shape, BF16),
+            pltpu.VMEM((2, 8, channels), F32),
+            pltpu.VMEM((2, 8, channels), F32),
+            pltpu.VMEM((8, 8, LANES), F32),
+            pltpu.VMEM((8, LANES), F32),
+            pltpu.VMEM((1, 8, channels), F32),
+            pltpu.VMEM((1, 8, channels), F32),
+            dma((4,)), dma((7,)), dma((8,)), dma((1,)), dma((1,)), dma, dma,
+            dma((4, len(PIECES))), dma((len(PIECES), 4)), dma((4,)), dma((2,)),
+        ],
+        compiler_params=params(0),
+        name="res_first",
+    )(x, time_emb, scale, shift, w, time_w)
+
+
+def second_call(count, tile_shape, a, stats, time_vec, scale, shift, w):
+    rows, cols, channels = a.shape
+    dma = pltpu.SemaphoreType.DMA
+    return pl.pallas_call(
+        functools.partial(second_kernel, count),
         out_shape=jax.ShapeDtypeStruct(tile_shape, BF16),
         in_specs=[ANY_SPEC, VMEM_SPEC, VMEM_SPEC, VMEM_SPEC, VMEM_SPEC, ANY_SPEC],
         out_specs=ANY_SPEC,
-        scratch_shapes=scratch + [pltpu.SemaphoreType.DMA],
+        scratch_shapes=conv_scratch(rows, cols, channels) + [
+            pltpu.VMEM((2, 8, channels), F32),
+            pltpu.VMEM((rows, cols, channels), BF16),
+            pltpu.VMEM((2, 8, channels), F32),
+            pltpu.VMEM((2, 8, channels), F32),
+            dma((3,)), dma((2,)), dma((2,)), dma((2,)), dma((2,)), dma((CHUNKS, 2)), dma((4, CHUNKS // 2)),
+        ],
         compiler_params=params(2),
         name="res_second",
-    )(*data, time_vec, scale, shift, w)
+    )(a, stats, time_vec, scale, shift, w)
 
 
 def attention_call(norm_idx, count, heads, a, stats, scale, shift, w, wo):
@@ -511,17 +699,11 @@
         rows, cols = 2 * tile_rows, 2 * tile_cols
         count = 2 * rows * cols * (channels // GROUPS)
         heads = w_out.shape[0]
-        chip_x, _, chip_y = position()
-        image = 2 * chip_x + chip_y
-        time_act = jax.nn.silu(time_emb.astype(F32)).astype(BF16)
-        time_vecs = jnp.einsum("bt,stc->sbc", time_act, time_w, preferred_element_type=F32)
-        time_vec = lax.dynamic_slice_in_dim(time_vecs, image, 1, axis=1)
-        w = conv_w.reshape(4, 3, 3 * channels, channels)
+        w = conv_w.reshape(4, 9 * channels, channels)
         qkv = jnp.transpose(w_qkv, (0, 2, 3, 1)).reshape(3, channels, channels)
         wo = w_out.reshape(channels, channels)
-        sizes = (count, rows, cols, channels, x.shape)
-        first, stats = res_call(True, 0, 0, *sizes, (x,), time_vec[0], gn_scale, gn_shift, w)
+        first, stats, time_vec = first_call(count, rows, cols, x, time_emb, gn_scale, gn_shift, w, time_w)
         middle, stats = attention_call(2, count, heads, first.reshape(rows * cols, channels), stats, gn_scale, gn_shift, qkv, wo)
-        return res_call(False, 3, 2, *sizes, (middle.reshape(rows, cols, channels), stats), time_vec[1], gn_scale, gn_shift, w)
+        return second_call(count, x.shape, middle.reshape(rows, cols, channels), stats, time_vec, gn_scale, gn_shift, w)
 
     return jax.shard_map(local, mesh=mesh, in_specs=(lat_spec, P("dp", None), P(), P(), P(), P(), P(), P()), out_specs=lat_spec, check_vma=False)

time: 269 us -> 227 us (0.84)
  Pallas kernels: 262 us -> 223 us
    pallas_call x2, Pallas kernels: 173 us -> 135 us  [the longest x1 73 us: first_call(): pl.pallas_call(functools.partial(first_kernel, count), out_shape=[jax.Sha...]
    unnamed x3 -> x1, local copies, waits for them, and re-layouts: 5.44 us -> 3.51 us
where the time goes in v3:
time: 227 us
  Pallas kernels  223 us (98%)
  local copies, waits for them, and re-layouts  3.51 us (2%)
    pallas_call x1, Pallas kernels, attention_call(): pl.pallas_call(functools.partial(attention_kernel, norm_idx, count, logit...  88 us
    pallas_call x1, Pallas kernels, first_call(): pl.pallas_call(functools.partial(first_kernel, count), out_shape=[jax.Sha...  73 us
    pallas_call x1, Pallas kernels, second_call(): pl.pallas_call(functools.partial(second_kernel, count), out_shape=jax.Sha...  62.1 us

profile of v3, /device:TPU:1, one launch (start us, length us, event | category | flops | bytes accessed | tf_op | source)
XLA Modules:
  0.0 226.7 jit_solution(7291939711398313995)
XLA Ops:
  0.0 73.0 %res_first.1 = (bf16[32,64,640]{2,1,0:T(8,128)(2,1)}, f32[8,640]{1,0:T(8,128)}, f32[8,640]{1,0:T(8,128)}) custom-call(bf16[4,16,32,640]{3,2,1,0:T(8,128)(2,1)} %x_ref.1, bf16[4,1280]{1,0:T(4,128)(2,1)} %emb_ref.1, bf16[5,640]{1,0:T(8,128)(2,1)} %scale_ref.5, bf16[5,640]{1,0:T(8,128)(2,1)} %shift_ref.5, bf16[4,5760,640]{2,1,0:T(8,128)(2,1)} %bitcast.7, ...), custom_call_target="tpu_custom_call" | custom-call | tf_op jit(solution)/shard_map/res_first/pallas_call | solution.py:611
  73.0 88.0 %attention.1 = (bf16[2048,640]{1,0:T(8,128)(2,1)}, f32[8,640]{1,0:T(8,128)}) custom-call(bf16[2048,640]{1,0:T(8,128)(2,1)} %bitcast.9, f32[8,640]{1,0:T(8,128)} %get-tuple-element.11.stat_in, bf16[5,640]{1,0:T(8,128)(2,1)} %scale_ref.5, bf16[5,640]{1,0:T(8,128)(2,1)} %shift_ref.5, bf16[3,640,640]{2,1,0:T(8,128)(2,1)} %bitcast.11, bf16[640,640]{1,0:T(8,128)(2,1)} %bitcast.12), custom_call_target="tpu_custom_call" | custom-call | tf_op jit(solution)/shard_map/attention/pallas_call | solution.py:660
  161.0 62.1 %res_second.1 = bf16[4,16,32,640]{3,2,1,0:T(8,128)(2,1)} custom-call(bf16[32,64,640]{2,1,0:T(8,128)(2,1)} %bitcast.10, f32[8,640]{1,0:T(8,128)} %get-tuple-element.13.stat_in, f32[8,640]{1,0:T(8,128)} %get-tuple-element.14.time_ref, bf16[5,640]{1,0:T(8,128)(2,1)} %scale_ref.5, bf16[5,640]{1,0:T(8,128)(2,1)} %shift_ref.5, bf16[4,5760,640]{2,1,0:T(8,128)(2,1)} %bitcast.8), custom_call_target="tpu_custom_call" | custom-call | tf_op jit(solution)/shard_map/res_second/pallas_call | solution.py:639
  223.2 3.5 %copy.10 = bf16[4,16,32,640]{3,2,1,0:T(8,128)(2,1)} copy(bf16[4,16,32,640]{3,2,1,0:T(8,128)(2,1)} %res_second.1) | data formatting | bytes 5242880

commit v4 on v3

--- a/solution.py
+++ b/solution.py
@@ -147,12 +147,17 @@
     return jnp.dot(lhs, w[...], preferred_element_type=F32)
 
 
-def conv_loop(order, ready, fill, finish, u_even, u_odd, w):
+def conv_loop(order, ready, fill, finish, u_even, u_odd, w, arriving=False):
     def step(i, half, parity, u_now, u_next):
         after = jnp.minimum(i + 1, CHUNKS - 1)
-        ready(half, parity)
-        fill(u_next, order(after))
-        finish(order(i), conv_chunk(u_now, w))
+        if arriving:
+            finish(order(i), conv_chunk(u_now, w))
+            ready(half, parity)
+            fill(u_next, order(after))
+        else:
+            ready(half, parity)
+            fill(u_next, order(after))
+            finish(order(i), conv_chunk(u_now, w))
 
     def pair(half, carry):
         step(2 * half, half, 0, u_even, u_odd)
@@ -202,28 +207,6 @@
     tw_load = pltpu.make_async_copy(tw_ref, tw_vmem, load_sem.at[3])
     for copy in weights[:1] + [tw_load] + weights[1:]:
         copy.start()
-
-    gather, spread = group_matrices(channels)
-    x_load.wait()
-    moments = []
-    for i in range(images):
-        acc_ref[...] = jnp.zeros_like(acc_ref)
-
-        def add_row(row, carry):
-            add_moments(acc_ref, x_vmem[i, row].astype(F32))
-            return carry
-
-        lax.fori_loop(0, tile_rows, add_row, 0)
-        moments += [jnp.sum(acc_ref[0], axis=0, keepdims=True), jnp.sum(acc_ref[1], axis=0, keepdims=True)]
-    grp_recv[me] = exact_dot(jnp.concatenate(moments, axis=0), gather)
-    wait_all()
-    group_copies = []
-    for k, (to_sp, to_y) in enumerate(others()):
-        copy = pltpu.make_async_remote_copy(
-            src_ref=grp_recv.at[me], dst_ref=grp_recv.at[me], send_sem=grp_ssem.at[k], recv_sem=grp_rsem.at[me],
-            device_id={"sp": to_sp, "sp2": to_y}, device_id_type=MESH)
-        copy.start()
-        group_copies.append((copy, 2 * to_sp + to_y))
 
     def piece(part, source_core):
         low, high = PIECES[part]
@@ -253,12 +236,7 @@
     at_home = core == chip_x
     far_first = (3, 2, 1, 0)
 
-    @pl.when(jnp.logical_not(at_home))
-    def _():
-        for k in far_first:
-            halo_copies(k)[0 if k else 1].start()
-
-    for part in range(len(PIECES)):
+    def send_piece(part):
         for k in far_first:
             remote, local = piece_copies(k, part)
             if k:
@@ -266,6 +244,39 @@
             else:
                 pl.when(at_home)(local.start)
                 pl.when(jnp.logical_not(at_home))(remote.start)
+
+    wait_all()
+
+    @pl.when(jnp.logical_not(at_home))
+    def _():
+        for k in far_first:
+            halo_copies(k)[0 if k else 1].start()
+
+    send_piece(0)
+
+    gather, spread = group_matrices(channels)
+    x_load.wait()
+    moments = []
+    for i in range(images):
+        acc_ref[...] = jnp.zeros_like(acc_ref)
+
+        def add_row(row, carry):
+            add_moments(acc_ref, x_vmem[i, row].astype(F32))
+            return carry
+
+        lax.fori_loop(0, tile_rows, add_row, 0)
+        moments += [jnp.sum(acc_ref[0], axis=0, keepdims=True), jnp.sum(acc_ref[1], axis=0, keepdims=True)]
+    grp_recv[me] = exact_dot(jnp.concatenate(moments, axis=0), gather)
+    group_copies = []
+    for k, (to_sp, to_y) in enumerate(others()):
+        copy = pltpu.make_async_remote_copy(
+            src_ref=grp_recv.at[me], dst_ref=grp_recv.at[me], send_sem=grp_ssem.at[k], recv_sem=grp_rsem.at[me],
+            device_id={"sp": to_sp, "sp2": to_y}, device_id_type=MESH)
+        copy.start()
+        group_copies.append((copy, 2 * to_sp + to_y))
+
+    for part in range(1, len(PIECES)):
+        send_piece(part)
 
     tw_load.wait()
     emb = silu(emb_ref[...].astype(F32)).astype(BF16)
@@ -317,7 +328,7 @@
         add_moments(acc_ref, hidden.astype(F32))
 
     conv_loop(from_ends, ready, lambda u_ref, chunk: fill_chunk(u_ref, a_ref, chunk, params, top_edge, bottom_edge),
-              finish_first, u_even, u_odd, w_vmem.at[0])
+              finish_first, u_even, u_odd, w_vmem.at[0], arriving=True)
 
     edge = send_edge_row(h_ref, edge_ssem, edge_rsem)
     edge.start()
@@ -473,19 +484,21 @@
     chunks = tokens // step
     transposed = (((1,), (1,)), ((), ()))
 
-    def kv_copy(which, chunk):
+    def head_copy(which, head, chunk=None):
+        first, size = (0, tokens) if chunk is None else (pl.multiple_of(chunk * step, step), step)
+        src, dst = pl.ds(first, size), pl.ds(tokens + first, size)
         if which:
-            ref, axis_index = v_ref, (slice(None), slice(None))
+            src_ref, dst_ref = v_ref.at[head, :, src], v_ref.at[head, :, dst]
         else:
-            ref, axis_index = k_ref, (slice(None),)
+            src_ref, dst_ref = k_ref.at[head, src], k_ref.at[head, dst]
+        slot = head if chunk is None else heads + chunk
         return pltpu.make_async_remote_copy(
-            src_ref=ref.at[axis_index + (pl.ds(pl.multiple_of(chunk * step, step), step),)],
-            dst_ref=ref.at[axis_index + (pl.ds(pl.multiple_of(tokens + chunk * step, step), step),)],
-            send_sem=kv_ssem.at[which, chunk],
-            recv_sem=kv_rsem.at[which, chunk],
-            device_id=partner_id(),
-            device_id_type=MESH,
-        )
+            src_ref=src_ref, dst_ref=dst_ref, send_sem=kv_ssem.at[which, slot], recv_sem=kv_rsem.at[which, slot],
+            device_id=partner_id(), device_id_type=MESH)
+
+    def both(act, head, chunk=None):
+        for which in range(2):
+            getattr(head_copy(which, head, chunk), act)()
 
     def key_values(i, carry):
         here = pl.ds(pl.multiple_of(i * step, step), step)
@@ -500,8 +513,7 @@
 
         @pl.when(i > 0)
         def _():
-            kv_copy(0, i - 1).start()
-            kv_copy(1, i - 1).start()
+            both("start", 0, i - 1)
         return carry
 
     lax.fori_loop(0, chunks, key_values, 0)
@@ -515,18 +527,15 @@
 
         @pl.when(i == 0)
         def _():
-            kv_copy(0, chunks - 1).start()
-            kv_copy(1, chunks - 1).start()
+            both("start", 0, chunks - 1)
+            for head in range(1, heads):
+                both("start", head)
         return carry
 
     lax.fori_loop(0, chunks, queries, 0)
 
-    def arrived(i, carry):
-        kv_copy(0, i).wait()
-        kv_copy(1, i).wait()
-        return carry
-
-    lax.fori_loop(0, chunks, arrived, 0)
+    for i in range(chunks):
+        both("wait_recv", 0, i)
 
     blocks = tokens // QUERY_BLOCK
     key_blocks = 2 * tokens // KEY_BLOCK
@@ -567,11 +576,17 @@
     interleaved(None, None, s_even, 1)
 
     def attend(i, carry):
+        head = lax.div(2 * i + 2, blocks)
+        pl.when((lax.rem(2 * i + 2, blocks) == 0) & (head < heads))(lambda: both("wait_recv", head))
         interleaved(2 * i, s_even, s_odd, 0)
         interleaved(2 * i + 1, s_odd, s_even, 1)
         return carry
 
     lax.fori_loop(0, heads * blocks // 2, attend, 0)
+    for i in range(chunks):
+        both("wait_send", 0, i)
+    for head in range(1, heads):
+        both("wait_send", head)
     loads[3].wait()
     acc_ref[...] = jnp.zeros_like(acc_ref)
 
@@ -683,8 +698,8 @@
             pltpu.SemaphoreType.DMA((heads,)),
             pltpu.SemaphoreType.DMA((1,)),
             pltpu.SemaphoreType.DMA((1,)),
-            pltpu.SemaphoreType.DMA((2, tokens // TOKEN_BLOCK)),
-            pltpu.SemaphoreType.DMA((2, tokens // TOKEN_BLOCK)),
+            pltpu.SemaphoreType.DMA((2, heads + tokens // TOKEN_BLOCK)),
+            pltpu.SemaphoreType.DMA((2, heads + tokens // TOKEN_BLOCK)),
         ],
         compiler_params=params(1),
         name="attention",

time: 227 us -> 217 us (0.956)
  Pallas kernels: 223 us -> 213 us
    pallas_call x1, Pallas kernels: 73 us -> 67.5 us  [first_call(): pl.pallas_call(functools.partial(first_kernel, count), out_shape=[jax.Sha...]
    pallas_call x1, Pallas kernels: 88 us -> 83.7 us  [attention_call(): pl.pallas_call(functools.partial(attention_kernel, norm_idx, count, logit...]
where the time goes in v4:
time: 217 us; the launch traced here: 216 us
  Pallas kernels  213 us (98%)
  local copies, waits for them, and re-layouts  3.51 us (2%)
    pallas_call x1, Pallas kernels, attention_call(): pl.pallas_call(functools.partial(attention_kernel, norm_idx, count, logit...  83.7 us
    pallas_call x1, Pallas kernels, first_call(): pl.pallas_call(functools.partial(first_kernel, count), out_shape=[jax.Sha...  67.5 us
    pallas_call x1, Pallas kernels, second_call(): pl.pallas_call(functools.partial(second_kernel, count), out_shape=jax.Sha...  61.6 us

profile of v4, /device:TPU:1, one launch (start us, length us, event | category | flops | bytes accessed | tf_op | source)
XLA Modules:
  0.0 216.3 jit_solution(1173509999104819516)
XLA Ops:
  0.0 67.5 %res_first.1 = (bf16[32,64,640]{2,1,0:T(8,128)(2,1)}, f32[8,640]{1,0:T(8,128)}, f32[8,640]{1,0:T(8,128)}) custom-call(bf16[4,16,32,640]{3,2,1,0:T(8,128)(2,1)} %x_ref.1, bf16[4,1280]{1,0:T(4,128)(2,1)} %emb_ref.1, bf16[5,640]{1,0:T(8,128)(2,1)} %scale_ref.5, bf16[5,640]{1,0:T(8,128)(2,1)} %shift_ref.5, bf16[4,5760,640]{2,1,0:T(8,128)(2,1)} %bitcast.7, ...), custom_call_target="tpu_custom_call" | custom-call | tf_op jit(solution)/shard_map/res_first/pallas_call | solution.py:626
  67.5 83.7 %attention.1 = (bf16[2048,640]{1,0:T(8,128)(2,1)}, f32[8,640]{1,0:T(8,128)}) custom-call(bf16[2048,640]{1,0:T(8,128)(2,1)} %bitcast.9, f32[8,640]{1,0:T(8,128)} %get-tuple-element.11.stat_in, bf16[5,640]{1,0:T(8,128)(2,1)} %scale_ref.5, bf16[5,640]{1,0:T(8,128)(2,1)} %shift_ref.5, bf16[3,640,640]{2,1,0:T(8,128)(2,1)} %bitcast.11, bf16[640,640]{1,0:T(8,128)(2,1)} %bitcast.12), custom_call_target="tpu_custom_call" | custom-call | tf_op jit(solution)/shard_map/attention/pallas_call | solution.py:675
  151.3 61.6 %res_second.1 = bf16[4,16,32,640]{3,2,1,0:T(8,128)(2,1)} custom-call(bf16[32,64,640]{2,1,0:T(8,128)(2,1)} %bitcast.10, f32[8,640]{1,0:T(8,128)} %get-tuple-element.13.stat_in, f32[8,640]{1,0:T(8,128)} %get-tuple-element.14.time_ref, bf16[5,640]{1,0:T(8,128)(2,1)} %scale_ref.5, bf16[5,640]{1,0:T(8,128)(2,1)} %shift_ref.5, bf16[4,5760,640]{2,1,0:T(8,128)(2,1)} %bitcast.8), custom_call_target="tpu_custom_call" | custom-call | tf_op jit(solution)/shard_map/res_second/pallas_call | solution.py:654
  212.8 3.5 %copy.10 = bf16[4,16,32,640]{3,2,1,0:T(8,128)(2,1)} copy(bf16[4,16,32,640]{3,2,1,0:T(8,128)(2,1)} %res_second.1) | data formatting | bytes 5242880

commit v5 on v4

--- a/solution.py
+++ b/solution.py
@@ -143,8 +143,14 @@
 
 def conv_chunk(u_ref, w):
     _, cols, depth = u_ref.shape
-    lhs = jnp.concatenate([u_ref[dy:dy + CHUNK_ROWS].reshape(CHUNK_ROWS * cols, depth) for dy in range(3)], axis=1)
-    return jnp.dot(lhs, w[...], preferred_element_type=F32)
+    rows, split = CHUNK_ROWS * cols, w.shape[1] - LANES
+    taps = [u_ref[dy:dy + CHUNK_ROWS].reshape(rows, depth) for dy in range(3)]
+    main = jnp.dot(jnp.concatenate(taps, axis=1), w[:, 0:split], preferred_element_type=F32)
+    both = jnp.concatenate([w[0:depth, split:], w[depth:2 * depth, split:]], axis=1)
+    pair = jnp.dot(u_ref[0:CHUNK_ROWS + 1].reshape(rows + cols, depth), both, preferred_element_type=F32)
+    third = jnp.dot(taps[2], w[2 * depth:, split:], preferred_element_type=F32)
+    rest = pair[0:rows, 0:LANES] + pair[cols:, LANES:] + third
+    return jnp.concatenate([main, rest], axis=1)
 
 
 def conv_loop(order, ready, fill, finish, u_even, u_odd, w, arriving=False):
@@ -205,8 +211,7 @@
     x_load.start()
     weights = [pltpu.make_async_copy(w_ref.at[k], w_vmem.at[k], load_sem.at[1 + k]) for k in range(2)]
     tw_load = pltpu.make_async_copy(tw_ref, tw_vmem, load_sem.at[3])
-    for copy in weights[:1] + [tw_load] + weights[1:]:
-        copy.start()
+    tw_load.start()
 
     def piece(part, source_core):
         low, high = PIECES[part]
@@ -253,6 +258,8 @@
             halo_copies(k)[0 if k else 1].start()
 
     send_piece(0)
+    for copy in weights:
+        copy.start()
 
     gather, spread = group_matrices(channels)
     x_load.wait()
@@ -454,7 +461,7 @@
 
 
 def attention_kernel(norm_idx, count, logit_scale, a_hbm, stat_in, scale_ref, shift_ref, w_hbm, wo_hbm,
-                     out_ref, stat_ref, a_ref, n_ref, q_ref, k_ref, v_ref, s_even, s_odd, peak_ref, o_ref,
+                     out_ref, stat_ref, a_ref, n_ref, q_ref, k_ref, v_ref, s_even, s_odd, peak_ref, total_ref, part_ref, o_ref,
                      wq_ref, wk_ref, wv_ref, wo_ref, acc_ref,
                      st_send, st_recv, load_sem, head_sem, st_ssem, st_rsem, kv_ssem, kv_rsem):
     tokens, channels = a_ref.shape
@@ -519,11 +526,15 @@
     lax.fori_loop(0, chunks, key_values, 0)
     loads[2].wait()
 
-    def queries(i, carry):
+    def query_chunk(i):
         here = pl.ds(pl.multiple_of(i * step, step), step)
         part = lax.dot_general(wq_ref[...], n_ref[here], transposed, preferred_element_type=F32).astype(BF16)
         for head in range(heads):
             q_ref[head, 0:head_dim, here] = part[head * head_dim:(head + 1) * head_dim]
+
+    def queries(i, carry):
+        query_chunk(2 * i)
+        query_chunk(2 * i + 1)
 
         @pl.when(i == 0)
         def _():
@@ -532,7 +543,7 @@
                 both("start", head)
         return carry
 
-    lax.fori_loop(0, chunks, queries, 0)
+    lax.fori_loop(0, chunks // 2, queries, 0)
 
     for i in range(chunks):
         both("wait_recv", 0, i)
@@ -543,46 +554,68 @@
     def fold(value, combine):
         return combine(value.reshape(KEY_BLOCK // 8, 8, QUERY_BLOCK), axis=0)
 
-    def interleaved(i, s_ref, s_next, slot):
-        if i is not None:
-            head = lax.div(i, blocks)
-            here = pl.ds(pl.multiple_of(lax.rem(i, blocks) * QUERY_BLOCK, QUERY_BLOCK), QUERY_BLOCK)
-            peak = jnp.max(peak_ref[slot], axis=0, keepdims=True)
-            after = jnp.minimum(i + 1, heads * blocks - 1)
-        else:
-            after = 0
-        next_head = lax.div(after, blocks)
-        next_here = pl.ds(pl.multiple_of(lax.rem(after, blocks) * QUERY_BLOCK, QUERY_BLOCK), QUERY_BLOCK)
+    def place_of(block):
+        first = pl.multiple_of(lax.rem(block, blocks) * QUERY_BLOCK, QUERY_BLOCK)
+        return lax.div(block, blocks), pl.ds(first, QUERY_BLOCK)
+
+    def keys_of(j):
+        return slice(j * KEY_BLOCK, (j + 1) * KEY_BLOCK)
+
+    def score(j, head, query, s_ref, peak):
+        scores = jnp.dot(k_ref[head, keys_of(j)], query, preferred_element_type=F32)
+        s_ref[keys_of(j)] = scores
+        piece = fold(scores, jnp.max)
+        return piece if peak is None else jnp.maximum(peak, piece)
+
+    def absorb(j, head, peak, s_ref, state):
+        weights = jnp.exp2((s_ref[keys_of(j)] - peak) * logit_scale)
+        total = fold(weights, jnp.sum)
+        attended = jnp.dot(v_ref[head, :, keys_of(j)], weights.astype(BF16), preferred_element_type=F32)
+        return (total, attended) if state is None else (state[0] + total, state[1] + attended)
+
+    def finish_block(block, peak, s_ref, state):
+        head, here = place_of(block)
+        total, attended = absorb(key_blocks - 1, head, peak, s_ref, state)
+        total = jnp.sum(total, axis=0, keepdims=True)
+        o_ref[pl.ds(pl.multiple_of(head * head_dim, 16), head_dim), here] = (attended / total).astype(BF16)
+
+    def peak_of(slot):
+        return jnp.max(peak_ref[slot], axis=0, keepdims=True)
+
+    def advance(i, s_ref, s_next, slot, state):
+        head, _ = place_of(i)
+        next_head, next_here = place_of(jnp.minimum(i + 1, heads * blocks - 1))
         query = q_ref[next_head, :, next_here]
-        next_peak, total, attended = None, None, None
+        peak, next_peak, new_state = peak_of(slot), None, None
         for j in range(key_blocks):
-            keys = slice(j * KEY_BLOCK, (j + 1) * KEY_BLOCK)
-            scores = jnp.dot(k_ref[next_head, keys], query, preferred_element_type=F32)
-            s_next[keys] = scores
-            piece = fold(scores, jnp.max)
-            next_peak = piece if next_peak is None else jnp.maximum(next_peak, piece)
-            if i is not None:
-                weights = jnp.exp2((s_ref[keys] - peak) * logit_scale)
-                piece = fold(weights, jnp.sum)
-                total = piece if total is None else total + piece
-                term = jnp.dot(v_ref[head, :, keys], weights.astype(BF16), preferred_element_type=F32)
-                attended = term if attended is None else attended + term
+            next_peak = score(j, next_head, query, s_next, next_peak)
+            if j == 1:
+                finish_block(jnp.maximum(i - 1, 0), peak_of(1 - slot), s_next, state)
+            if j:
+                new_state = absorb(j - 1, head, peak, s_ref, new_state)
         peak_ref[1 - slot] = next_peak
-        if i is not None:
-            total = jnp.sum(total, axis=0, keepdims=True)
-            rows = pl.ds(pl.multiple_of(head * head_dim, 16), head_dim)
-            o_ref[rows, here] = (attended / total).astype(BF16)
-
-    interleaved(None, None, s_even, 1)
+        return new_state
+
+    s_odd[keys_of(key_blocks - 1)] = jnp.zeros((KEY_BLOCK, QUERY_BLOCK), F32)
+    peak_ref[1] = jnp.zeros((8, QUERY_BLOCK), F32)
+    total_ref[...] = jnp.zeros_like(total_ref)
+    part_ref[...] = jnp.zeros_like(part_ref)
+    query = q_ref[0, :, 0:QUERY_BLOCK]
+    first_peak = None
+    for j in range(key_blocks):
+        first_peak = score(j, 0, query, s_even, first_peak)
+    peak_ref[0] = first_peak
 
     def attend(i, carry):
         head = lax.div(2 * i + 2, blocks)
         pl.when((lax.rem(2 * i + 2, blocks) == 0) & (head < heads))(lambda: both("wait_recv", head))
-        interleaved(2 * i, s_even, s_odd, 0)
-        interleaved(2 * i + 1, s_odd, s_even, 1)
+        state = advance(2 * i, s_even, s_odd, 0, (total_ref[...], part_ref[...]))
+        state = advance(2 * i + 1, s_odd, s_even, 1, state)
+        total_ref[...], part_ref[...] = state
         return carry
 
     lax.fori_loop(0, heads * blocks // 2, attend, 0)
+    finish_block(jnp.int32(heads * blocks - 1), peak_of(1), s_odd, (total_ref[...], part_ref[...]))
     for i in range(chunks):
         both("wait_send", 0, i)
     for head in range(1, heads):
@@ -590,16 +623,28 @@
     loads[3].wait()
     acc_ref[...] = jnp.zeros_like(acc_ref)
 
-    def project(i, carry):
+    def project_chunk(i):
         here = pl.ds(pl.multiple_of(i * step, step), step)
         added = lax.dot_general(o_ref[:, here], wo_ref[...], (((0,), (0,)), ((), ())), preferred_element_type=F32)
         new = (a_ref[here].astype(F32) + added).astype(BF16)
-        out_ref[here] = new
+        a_ref[here] = new
         add_moments(acc_ref, new.astype(F32))
+
+    def leave(i):
+        here = pl.ds(pl.multiple_of(i * 2 * step, 2 * step), 2 * step)
+        return pltpu.make_async_copy(a_ref.at[here], out_ref.at[here], load_sem.at[i])
+
+    def project(i, carry):
+        pl.when(i > 0)(lambda: leave(i - 1).start())
+        project_chunk(2 * i)
+        project_chunk(2 * i + 1)
         return carry
 
-    lax.fori_loop(0, chunks, project, 0)
+    lax.fori_loop(0, chunks // 2, project, 0)
     stat_ref[...] = moment_rows(acc_ref)
+    leave(chunks // 2 - 1).start()
+    for i in range(chunks // 2):
+        leave(i).wait()
 
 
 VMEM_SPEC = pl.BlockSpec(memory_space=pltpu.VMEM)
@@ -676,7 +721,7 @@
         functools.partial(attention_kernel, norm_idx, count, logit_scale),
         out_shape=[jax.ShapeDtypeStruct((tokens, channels), BF16), jax.ShapeDtypeStruct((8, channels), F32)],
         in_specs=[ANY_SPEC, VMEM_SPEC, VMEM_SPEC, VMEM_SPEC, ANY_SPEC, ANY_SPEC],
-        out_specs=[VMEM_SPEC, VMEM_SPEC],
+        out_specs=[ANY_SPEC, VMEM_SPEC],
         scratch_shapes=[
             pltpu.VMEM((tokens, channels), BF16),
             pltpu.VMEM((tokens, channels), BF16),
@@ -686,6 +731,8 @@
             pltpu.VMEM((2 * tokens, QUERY_BLOCK), F32),
             pltpu.VMEM((2 * tokens, QUERY_BLOCK), F32),
             pltpu.VMEM((2, 8, QUERY_BLOCK), F32),
+            pltpu.VMEM((8, QUERY_BLOCK), F32),
+            pltpu.VMEM((head_dim, QUERY_BLOCK), F32),
             pltpu.VMEM((channels, tokens), BF16),
             pltpu.VMEM((channels, channels), BF16),
             pltpu.VMEM((heads * LANES, channels), BF16),

time: 217 us -> 211 us (0.972)
  Pallas kernels: 213 us -> 208 us
    pallas_call x1, Pallas kernels: 83.7 us -> 80.9 us  [attention_call(): pl.pallas_call(functools.partial(attention_kernel, norm_idx, count, logit...]
where the time goes in v5:
time: 211 us
  Pallas kernels  208 us (99%)
  local copies, waits for them, and re-layouts  3.51 us (2%)
    pallas_call x1, Pallas kernels, attention_call(): pl.pallas_call(functools.partial(attention_kernel, norm_idx, count, logit...  80.9 us
    pallas_call x1, Pallas kernels, first_call(): pl.pallas_call(functools.partial(first_kernel, count), out_shape=[jax.Sha...  66.2 us
    pallas_call x1, Pallas kernels, second_call(): pl.pallas_call(functools.partial(second_kernel, count), out_shape=jax.Sha...  60.5 us

profile of v5, /device:TPU:1, one launch (start us, length us, event | category | flops | bytes accessed | tf_op | source)
XLA Modules:
  0.0 211.1 jit_solution(4882722137354994074)
XLA Ops:
  0.0 66.2 %res_first.1 = (bf16[32,64,640]{2,1,0:T(8,128)(2,1)}, f32[8,640]{1,0:T(8,128)}, f32[8,640]{1,0:T(8,128)}) custom-call(bf16[4,16,32,640]{3,2,1,0:T(8,128)(2,1)} %x_ref.1, bf16[4,1280]{1,0:T(4,128)(2,1)} %emb_ref.1, bf16[5,640]{1,0:T(8,128)(2,1)} %scale_ref.5, bf16[5,640]{1,0:T(8,128)(2,1)} %shift_ref.5, bf16[4,5760,640]{2,1,0:T(8,128)(2,1)} %bitcast.7, ...), custom_call_target="tpu_custom_call" | custom-call | tf_op jit(solution)/shard_map/res_first/pallas_call | solution.py:671
  66.2 80.9 %attention.1 = (bf16[2048,640]{1,0:T(8,128)(2,1)}, f32[8,640]{1,0:T(8,128)}) custom-call(bf16[2048,640]{1,0:T(8,128)(2,1)} %bitcast.9, f32[8,640]{1,0:T(8,128)} %get-tuple-element.11.stat_in, bf16[5,640]{1,0:T(8,128)(2,1)} %scale_ref.5, bf16[5,640]{1,0:T(8,128)(2,1)} %shift_ref.5, bf16[3,640,640]{2,1,0:T(8,128)(2,1)} %bitcast.11, bf16[640,640]{1,0:T(8,128)(2,1)} %bitcast.12), custom_call_target="tpu_custom_call" | custom-call | tf_op jit(solution)/shard_map/attention/pallas_call | solution.py:720
  147.1 60.5 %res_second.1 = bf16[4,16,32,640]{3,2,1,0:T(8,128)(2,1)} custom-call(bf16[32,64,640]{2,1,0:T(8,128)(2,1)} %bitcast.10, f32[8,640]{1,0:T(8,128)} %get-tuple-element.13.stat_in, f32[8,640]{1,0:T(8,128)} %get-tuple-element.14.time_ref, bf16[5,640]{1,0:T(8,128)(2,1)} %scale_ref.5, bf16[5,640]{1,0:T(8,128)(2,1)} %shift_ref.5, bf16[4,5760,640]{2,1,0:T(8,128)(2,1)} %bitcast.8), custom_call_target="tpu_custom_call" | custom-call | tf_op jit(solution)/shard_map/res_second/pallas_call | solution.py:699
  207.5 3.5 %copy.10 = bf16[4,16,32,640]{3,2,1,0:T(8,128)(2,1)} copy(bf16[4,16,32,640]{3,2,1,0:T(8,128)(2,1)} %res_second.1) | data formatting | bytes 5242880

commit v6 on v5

--- a/solution.py
+++ b/solution.py
@@ -463,18 +463,15 @@
 def attention_kernel(norm_idx, count, logit_scale, a_hbm, stat_in, scale_ref, shift_ref, w_hbm, wo_hbm,
                      out_ref, stat_ref, a_ref, n_ref, q_ref, k_ref, v_ref, s_even, s_odd, peak_ref, total_ref, part_ref, o_ref,
                      wq_ref, wk_ref, wv_ref, wo_ref, acc_ref,
-                     st_send, st_recv, load_sem, head_sem, st_ssem, st_rsem, kv_ssem, kv_rsem):
+                     st_send, st_recv, load_sem, st_ssem, st_rsem, kv_ssem, kv_rsem):
     tokens, channels = a_ref.shape
     heads, head_dim, _ = v_ref.shape
-    loads = [pltpu.make_async_copy(src, dst, load_sem.at[i])
-             for i, (src, dst) in enumerate(((a_hbm, a_ref), (w_hbm.at[2], wv_ref), (w_hbm.at[0], wq_ref), (wo_hbm, wo_ref)))]
-    head_loads = [pltpu.make_async_copy(w_hbm.at[1, pl.ds(head * head_dim, head_dim)],
-                                        wk_ref.at[pl.ds(head * LANES, head_dim)], head_sem.at[head])
-                  for head in range(heads)]
-    for load in loads[:2] + head_loads + loads[2:]:
+    pairs = ((a_hbm, a_ref), (w_hbm.at[1], wk_ref), (w_hbm.at[2], wv_ref), (w_hbm.at[0], wq_ref), (wo_hbm, wo_ref))
+    loads = [pltpu.make_async_copy(src, dst, load_sem.at[i]) for i, (src, dst) in enumerate(pairs)]
+    for load in loads:
         load.start()
     for head in range(heads):
-        wk_ref[head * LANES + head_dim:(head + 1) * LANES] = jnp.zeros((LANES - head_dim, channels), BF16)
+        k_ref[head, 0:tokens, head_dim:] = jnp.zeros((tokens, LANES - head_dim), BF16)
         q_ref[head, head_dim:] = jnp.zeros((LANES - head_dim, tokens), BF16)
     st_send[0] = stat_in[...]
     barrier_pair()
@@ -482,9 +479,7 @@
     mean, inv_std = norm_params(sums, count)
     gain = inv_std * scale_ref[norm_idx:norm_idx + 1].astype(F32)
     shift = shift_ref[norm_idx:norm_idx + 1].astype(F32)
-    loads[0].wait()
-    loads[1].wait()
-    for load in head_loads:
+    for load in loads[:3]:
         load.wait()
 
     step = TOKEN_BLOCK
@@ -513,7 +508,7 @@
         n_ref[here] = normed
         part = lax.dot_general(normed, wk_ref[...], transposed, preferred_element_type=F32).astype(BF16)
         for head in range(heads):
-            k_ref[head, here] = part[:, head * LANES:(head + 1) * LANES]
+            k_ref[head, here, 0:head_dim] = part[:, head * head_dim:(head + 1) * head_dim]
         part = lax.dot_general(wv_ref[...], normed, transposed, preferred_element_type=F32).astype(BF16)
         for head in range(heads):
             v_ref[head, :, here] = part[head * head_dim:(head + 1) * head_dim]
@@ -524,7 +519,7 @@
         return carry
 
     lax.fori_loop(0, chunks, key_values, 0)
-    loads[2].wait()
+    loads[3].wait()
 
     def query_chunk(i):
         here = pl.ds(pl.multiple_of(i * step, step), step)
@@ -606,21 +601,22 @@
         first_peak = score(j, 0, query, s_even, first_peak)
     peak_ref[0] = first_peak
 
-    def attend(i, carry):
-        head = lax.div(2 * i + 2, blocks)
-        pl.when((lax.rem(2 * i + 2, blocks) == 0) & (head < heads))(lambda: both("wait_recv", head))
-        state = advance(2 * i, s_even, s_odd, 0, (total_ref[...], part_ref[...]))
-        state = advance(2 * i + 1, s_odd, s_even, 1, state)
+    def attend(head, carry):
+        pl.when(head + 1 < heads)(lambda: both("wait_recv", head + 1))
+        state = (total_ref[...], part_ref[...])
+        for j in range(0, blocks, 2):
+            state = advance(blocks * head + j, s_even, s_odd, 0, state)
+            state = advance(blocks * head + j + 1, s_odd, s_even, 1, state)
         total_ref[...], part_ref[...] = state
         return carry
 
-    lax.fori_loop(0, heads * blocks // 2, attend, 0)
+    lax.fori_loop(0, heads, attend, 0)
     finish_block(jnp.int32(heads * blocks - 1), peak_of(1), s_odd, (total_ref[...], part_ref[...]))
     for i in range(chunks):
         both("wait_send", 0, i)
     for head in range(1, heads):
         both("wait_send", head)
-    loads[3].wait()
+    loads[4].wait()
     acc_ref[...] = jnp.zeros_like(acc_ref)
 
     def project_chunk(i):
@@ -713,6 +709,31 @@
     )(a, stats, time_vec, scale, shift, w)
 
 
+def copy_kernel(src_ref, out_ref, buf_ref, in_sem, out_sem):
+    parts = [(i, slice(j * 8, (j + 1) * 8)) for i in range(src_ref.shape[0]) for j in range(src_ref.shape[1] // 8)]
+    reads = [pltpu.make_async_copy(src_ref.at[i, rows], buf_ref.at[i, rows], in_sem.at[n]) for n, (i, rows) in enumerate(parts)]
+    writes = [pltpu.make_async_copy(buf_ref.at[i, rows], out_ref.at[i, rows], out_sem.at[n]) for n, (i, rows) in enumerate(parts)]
+    for read in reads:
+        read.start()
+    for read, write in zip(reads, writes):
+        read.wait()
+        write.start()
+    for write in writes:
+        write.wait()
+
+
+def copy_call(src):
+    parts = src.shape[0] * (src.shape[1] // 8)
+    return pl.pallas_call(
+        copy_kernel,
+        out_shape=jax.ShapeDtypeStruct(src.shape, src.dtype),
+        in_specs=[ANY_SPEC],
+        out_specs=ANY_SPEC,
+        scratch_shapes=[pltpu.VMEM(src.shape, src.dtype), pltpu.SemaphoreType.DMA((parts,)), pltpu.SemaphoreType.DMA((parts,))],
+        name="copy_out",
+    )(src)
+
+
 def attention_call(norm_idx, count, heads, a, stats, scale, shift, w, wo):
     tokens, channels = a.shape
     head_dim = channels // heads
@@ -735,14 +756,13 @@
             pltpu.VMEM((head_dim, QUERY_BLOCK), F32),
             pltpu.VMEM((channels, tokens), BF16),
             pltpu.VMEM((channels, channels), BF16),
-            pltpu.VMEM((heads * LANES, channels), BF16),
+            pltpu.VMEM((channels, channels), BF16),
             pltpu.VMEM((channels, channels), BF16),
             pltpu.VMEM((channels, channels), BF16),
             pltpu.VMEM((2, 8, channels), F32),
             pltpu.VMEM((1, 8, channels), F32),
             pltpu.VMEM((1, 8, channels), F32),
-            pltpu.SemaphoreType.DMA((4,)),
-            pltpu.SemaphoreType.DMA((heads,)),
+            pltpu.SemaphoreType.DMA((5,)),
             pltpu.SemaphoreType.DMA((1,)),
             pltpu.SemaphoreType.DMA((1,)),
             pltpu.SemaphoreType.DMA((2, heads + tokens // TOKEN_BLOCK)),
@@ -766,6 +786,6 @@
         wo = w_out.reshape(channels, channels)
         first, stats, time_vec = first_call(count, rows, cols, x, time_emb, gn_scale, gn_shift, w, time_w)
         middle, stats = attention_call(2, count, heads, first.reshape(rows * cols, channels), stats, gn_scale, gn_shift, qkv, wo)
-        return second_call(count, x.shape, middle.reshape(rows, cols, channels), stats, time_vec, gn_scale, gn_shift, w)
+        return copy_call(second_call(count, x.shape, middle.reshape(rows, cols, channels), stats, time_vec, gn_scale, gn_shift, w))
 
     return jax.shard_map(local, mesh=mesh, in_specs=(lat_spec, P("dp", None), P(), P(), P(), P(), P(), P()), out_specs=lat_spec, check_vma=False)

time: 211 us -> 209 us (level)
  local copies, waits for them, and re-layouts: 3.51 us -> 0 us
    unnamed x1 -> x0, local copies, waits for them, and re-layouts: 3.51 us -> none
    pallas_call x0 -> x1, Pallas kernels: none -> 2.59 us  [copy_call(): pl.pallas_call(copy_kernel, out_shape=jax.ShapeDtypeStruct(src.shape, src...]
where the time goes in v6:
time: 209 us
  Pallas kernels  209 us (100%)
    pallas_call x1, Pallas kernels, attention_call(): pl.pallas_call(functools.partial(attention_kernel, norm_idx, count, logit...  79.6 us
    pallas_call x1, Pallas kernels, first_call(): pl.pallas_call(functools.partial(first_kernel, count), out_shape=[jax.Sha...  66.2 us
    pallas_call x1, Pallas kernels, second_call(): pl.pallas_call(functools.partial(second_kernel, count), out_shape=jax.Sha...  60.2 us

profile of v6, /device:TPU:1, one launch (start us, length us, event | category | flops | bytes accessed | tf_op | source)
XLA Modules:
  0.0 208.9 jit_solution(16573530878630593062)
XLA Ops:
  0.0 66.2 %res_first.1 = (bf16[32,64,640]{2,1,0:T(8,128)(2,1)}, f32[8,640]{1,0:T(8,128)}, f32[8,640]{1,0:T(8,128)}) custom-call(bf16[4,16,32,640]{3,2,1,0:T(8,128)(2,1)} %x_ref.1, bf16[4,1280]{1,0:T(4,128)(2,1)} %emb_ref.1, bf16[5,640]{1,0:T(8,128)(2,1)} %scale_ref.5, bf16[5,640]{1,0:T(8,128)(2,1)} %shift_ref.5, bf16[4,5760,640]{2,1,0:T(8,128)(2,1)} %bitcast.7, ...), custom_call_target="tpu_custom_call" | custom-call | tf_op jit(solution)/shard_map/res_first/pallas_call | solution.py:667
  66.2 79.6 %attention.1 = (bf16[2048,640]{1,0:T(8,128)(2,1)}, f32[8,640]{1,0:T(8,128)}) custom-call(bf16[2048,640]{1,0:T(8,128)(2,1)} %bitcast.9, f32[8,640]{1,0:T(8,128)} %get-tuple-element.11.stat_in, bf16[5,640]{1,0:T(8,128)(2,1)} %scale_ref.5, bf16[5,640]{1,0:T(8,128)(2,1)} %shift_ref.5, bf16[3,640,640]{2,1,0:T(8,128)(2,1)} %bitcast.11, bf16[640,640]{1,0:T(8,128)(2,1)} %bitcast.12), custom_call_target="tpu_custom_call" | custom-call | tf_op jit(solution)/shard_map/attention/pallas_call | solution.py:741
  145.8 60.2 %res_second.1.src_ref = bf16[4,16,32,640]{3,2,1,0:T(8,128)(2,1)} custom-call(bf16[32,64,640]{2,1,0:T(8,128)(2,1)} %bitcast.10, f32[8,640]{1,0:T(8,128)} %get-tuple-element.13.stat_in, f32[8,640]{1,0:T(8,128)} %get-tuple-element.14.time_ref, bf16[5,640]{1,0:T(8,128)(2,1)} %scale_ref.5, bf16[5,640]{1,0:T(8,128)(2,1)} %shift_ref.5, bf16[4,5760,640]{2,1,0:T(8,128)(2,1)} %bitcast.8), custom_call_target="tpu_custom_call" | custom-call | tf_op jit(solution)/shard_map/res_second/pallas_call | solution.py:695
  206.1 2.6 %copy_out.1 = bf16[4,16,32,640]{3,2,1,0:T(8,128)(2,1)} custom-call(bf16[4,16,32,640]{3,2,1,0:T(8,128)(2,1)} %res_second.1.src_ref), custom_call_target="tpu_custom_call" | custom-call | tf_op jit(solution)/shard_map/copy_out/pallas_call | solution.py:727

commit v7 on v6

--- a/solution.py
+++ b/solution.py
@@ -104,7 +104,7 @@
     return jnp.concatenate([total, square, jnp.zeros((6, total.shape[1]), F32)], axis=0)
 
 
-def exchange(slot, send_ref, recv_ref, send_sem, recv_sem):
+def exchange(slot, send_ref, recv_ref, send_sem, recv_sem, meanwhile=None):
     copy = pltpu.make_async_remote_copy(
         src_ref=send_ref.at[slot],
         dst_ref=recv_ref.at[slot],
@@ -114,6 +114,8 @@
         device_id_type=MESH,
     )
     copy.start()
+    if meanwhile is not None:
+        meanwhile()
     copy.wait()
     return send_ref[slot] + recv_ref[slot]
 
@@ -308,13 +310,12 @@
             pltpu.make_async_copy(landed, landed, piece_rsem.at[part, 2 * col + source_core]).wait()
 
     def ready(half, parity):
-        if parity == 0:
-            for part in range(3):
-                pl.when(half == part)(functools.partial(wait_piece, part, 1))
-        else:
-            for part in range(1, 4):
-                pl.when(half + 1 == part)(functools.partial(wait_piece, part, 0))
-            pl.when(half + 1 == 3)(functools.partial(wait_piece, 3, 1))
+        if parity:
+            for part in range(1, len(PIECES)):
+                @pl.when(half + 1 == part)
+                def _():
+                    wait_piece(part, 0)
+                    wait_piece(part, 1)
 
     top_edge, bottom_edge = core == 0, core == 1
 
@@ -326,6 +327,7 @@
         landed = a_ref.at[(rows + 1) * (1 - core), pl.ds(col * tile_cols, tile_cols)]
         pltpu.make_async_copy(landed, landed, halo_rsem.at[col]).wait()
     wait_piece(0, 0)
+    wait_piece(0, 1)
     acc_ref[...] = jnp.zeros_like(acc_ref)
     weights[0].wait()
 
@@ -470,12 +472,15 @@
     loads = [pltpu.make_async_copy(src, dst, load_sem.at[i]) for i, (src, dst) in enumerate(pairs)]
     for load in loads:
         load.start()
-    for head in range(heads):
-        k_ref[head, 0:tokens, head_dim:] = jnp.zeros((tokens, LANES - head_dim), BF16)
-        q_ref[head, head_dim:] = jnp.zeros((LANES - head_dim, tokens), BF16)
+
+    def clear_padding():
+        for head in range(heads):
+            k_ref[head, 0:tokens, head_dim:] = jnp.zeros((tokens, LANES - head_dim), BF16)
+            q_ref[head, head_dim:] = jnp.zeros((LANES - head_dim, tokens), BF16)
+
     st_send[0] = stat_in[...]
     barrier_pair()
-    sums = exchange(0, st_send, st_recv, st_ssem, st_rsem)
+    sums = exchange(0, st_send, st_recv, st_ssem, st_rsem, clear_padding)
     mean, inv_std = norm_params(sums, count)
     gain = inv_std * scale_ref[norm_idx:norm_idx + 1].astype(F32)
     shift = shift_ref[norm_idx:norm_idx + 1].astype(F32)
@@ -584,7 +589,7 @@
         peak, next_peak, new_state = peak_of(slot), None, None
         for j in range(key_blocks):
             next_peak = score(j, next_head, query, s_next, next_peak)
-            if j == 1:
+            if j == 0:
                 finish_block(jnp.maximum(i - 1, 0), peak_of(1 - slot), s_next, state)
             if j:
                 new_state = absorb(j - 1, head, peak, s_ref, new_state)

time: 209 us -> 208 us (level)
  no operation moved by 1% of the time
where the time goes in v7:
time: 208 us
  Pallas kernels  208 us (100%)
    pallas_call x1, Pallas kernels, attention_call(): pl.pallas_call(functools.partial(attention_kernel, norm_idx, count, logit...  79.2 us
    pallas_call x1, Pallas kernels, first_call(): pl.pallas_call(functools.partial(first_kernel, count), out_shape=[jax.Sha...  65.5 us
    pallas_call x1, Pallas kernels, second_call(): pl.pallas_call(functools.partial(second_kernel, count), out_shape=jax.Sha...  60.3 us

profile of v7, /device:TPU:1, one launch (start us, length us, event | category | flops | bytes accessed | tf_op | source)
XLA Modules:
  0.0 207.8 jit_solution(15562187775976326768)
XLA Ops:
  0.0 65.5 %res_first.1 = (bf16[32,64,640]{2,1,0:T(8,128)(2,1)}, f32[8,640]{1,0:T(8,128)}, f32[8,640]{1,0:T(8,128)}) custom-call(bf16[4,16,32,640]{3,2,1,0:T(8,128)(2,1)} %x_ref.1, bf16[4,1280]{1,0:T(4,128)(2,1)} %emb_ref.1, bf16[5,640]{1,0:T(8,128)(2,1)} %scale_ref.5, bf16[5,640]{1,0:T(8,128)(2,1)} %shift_ref.5, bf16[4,5760,640]{2,1,0:T(8,128)(2,1)} %bitcast.7, ...), custom_call_target="tpu_custom_call" | custom-call | tf_op jit(solution)/shard_map/res_first/pallas_call | solution.py:672
  65.5 79.2 %attention.1 = (bf16[2048,640]{1,0:T(8,128)(2,1)}, f32[8,640]{1,0:T(8,128)}) custom-call(bf16[2048,640]{1,0:T(8,128)(2,1)} %bitcast.9, f32[8,640]{1,0:T(8,128)} %get-tuple-element.11.stat_in, bf16[5,640]{1,0:T(8,128)(2,1)} %scale_ref.5, bf16[5,640]{1,0:T(8,128)(2,1)} %shift_ref.5, bf16[3,640,640]{2,1,0:T(8,128)(2,1)} %bitcast.11, bf16[640,640]{1,0:T(8,128)(2,1)} %bitcast.12), custom_call_target="tpu_custom_call" | custom-call | tf_op jit(solution)/shard_map/attention/pallas_call | solution.py:746
  144.7 60.3 %res_second.1.src_ref = bf16[4,16,32,640]{3,2,1,0:T(8,128)(2,1)} custom-call(bf16[32,64,640]{2,1,0:T(8,128)(2,1)} %bitcast.10, f32[8,640]{1,0:T(8,128)} %get-tuple-element.13.stat_in, f32[8,640]{1,0:T(8,128)} %get-tuple-element.14.time_ref, bf16[5,640]{1,0:T(8,128)(2,1)} %scale_ref.5, bf16[5,640]{1,0:T(8,128)(2,1)} %shift_ref.5, bf16[4,5760,640]{2,1,0:T(8,128)(2,1)} %bitcast.8), custom_call_target="tpu_custom_call" | custom-call | tf_op jit(solution)/shard_map/res_second/pallas_call | solution.py:700
  205.0 2.6 %copy_out.1 = bf16[4,16,32,640]{3,2,1,0:T(8,128)(2,1)} custom-call(bf16[4,16,32,640]{3,2,1,0:T(8,128)(2,1)} %res_second.1.src_ref), custom_call_target="tpu_custom_call" | custom-call | tf_op jit(solution)/shard_map/copy_out/pallas_call | solution.py:732

commit v8 on v7

--- a/solution.py
+++ b/solution.py
@@ -276,6 +276,13 @@
         lax.fori_loop(0, tile_rows, add_row, 0)
         moments += [jnp.sum(acc_ref[0], axis=0, keepdims=True), jnp.sum(acc_ref[1], axis=0, keepdims=True)]
     grp_recv[me] = exact_dot(jnp.concatenate(moments, axis=0), gather)
+    tw_load.wait()
+    emb = silu(emb_ref[...].astype(F32)).astype(BF16)
+    for k in range(2):
+        time_all[k, 0:images] = jnp.dot(emb, tw_vmem[k], preferred_element_type=F32)
+    time_ref[...] = jnp.broadcast_to(time_all[1, pl.ds(image, 1)], time_ref.shape)
+    time_vec = time_all[0, pl.ds(image, 1)]
+
     group_copies = []
     for k, (to_sp, to_y) in enumerate(others()):
         copy = pltpu.make_async_remote_copy(
@@ -286,13 +293,6 @@
 
     for part in range(1, len(PIECES)):
         send_piece(part)
-
-    tw_load.wait()
-    emb = silu(emb_ref[...].astype(F32)).astype(BF16)
-    for k in range(2):
-        time_all[k, 0:images] = jnp.dot(emb, tw_vmem[k], preferred_element_type=F32)
-    time_ref[...] = jnp.broadcast_to(time_all[1, pl.ds(image, 1)], time_ref.shape)
-    time_vec = time_all[0, pl.ds(image, 1)]
 
     total = jnp.zeros((8, LANES), F32)
     for copy, _ in group_copies:
@@ -340,8 +340,8 @@
               finish_first, u_even, u_odd, w_vmem.at[0], arriving=True)
 
     edge = send_edge_row(h_ref, edge_ssem, edge_rsem)
+    st_send[0] = moment_rows(acc_ref)
     edge.start()
-    st_send[0] = moment_rows(acc_ref)
     acc_ref[...] = jnp.zeros_like(acc_ref)
     weights[1].wait()
     second = norm(1, *norm_params(exchange(0, st_send, st_recv, st_ssem, st_rsem), count))
@@ -413,8 +413,8 @@
               finish_first, u_even, u_odd, w_vmem.at[0])
 
     edge = send_edge_row(h_ref, edge_ssem.at[1], edge_rsem.at[1])
+    st_send[1] = moment_rows(acc_ref)
     edge.start()
-    st_send[1] = moment_rows(acc_ref)
     weights[1].wait()
     second = norm(1, exchange(1, st_send, st_recv, st_ssem, st_rsem))
     edge.wait()

time: 208 us -> 208 us (level)
  no operation moved by 1% of the time
where the time goes in v8:
time: 208 us
  Pallas kernels  208 us (100%)
    pallas_call x1, Pallas kernels, attention_call(): pl.pallas_call(functools.partial(attention_kernel, norm_idx, count, logit...  79.2 us
    pallas_call x1, Pallas kernels, first_call(): pl.pallas_call(functools.partial(first_kernel, count), out_shape=[jax.Sha...  65.5 us
    pallas_call x1, Pallas kernels, second_call(): pl.pallas_call(functools.partial(second_kernel, count), out_shape=jax.Sha...  60.3 us

profile of v8, /device:TPU:1, one launch (start us, length us, event | category | flops | bytes accessed | tf_op | source)
XLA Modules:
  0.0 207.8 jit_solution(13396330564709274826)
XLA Ops:
  0.0 65.5 %res_first.1 = (bf16[32,64,640]{2,1,0:T(8,128)(2,1)}, f32[8,640]{1,0:T(8,128)}, f32[8,640]{1,0:T(8,128)}) custom-call(bf16[4,16,32,640]{3,2,1,0:T(8,128)(2,1)} %x_ref.1, bf16[4,1280]{1,0:T(4,128)(2,1)} %emb_ref.1, bf16[5,640]{1,0:T(8,128)(2,1)} %scale_ref.5, bf16[5,640]{1,0:T(8,128)(2,1)} %shift_ref.5, bf16[4,5760,640]{2,1,0:T(8,128)(2,1)} %bitcast.7, ...), custom_call_target="tpu_custom_call" | custom-call | tf_op jit(solution)/shard_map/res_first/pallas_call | solution.py:672
  65.5 79.2 %attention.1 = (bf16[2048,640]{1,0:T(8,128)(2,1)}, f32[8,640]{1,0:T(8,128)}) custom-call(bf16[2048,640]{1,0:T(8,128)(2,1)} %bitcast.9, f32[8,640]{1,0:T(8,128)} %get-tuple-element.11.stat_in, bf16[5,640]{1,0:T(8,128)(2,1)} %scale_ref.5, bf16[5,640]{1,0:T(8,128)(2,1)} %shift_ref.5, bf16[3,640,640]{2,1,0:T(8,128)(2,1)} %bitcast.11, bf16[640,640]{1,0:T(8,128)(2,1)} %bitcast.12), custom_call_target="tpu_custom_call" | custom-call | tf_op jit(solution)/shard_map/attention/pallas_call | solution.py:746
  144.7 60.3 %res_second.1.src_ref = bf16[4,16,32,640]{3,2,1,0:T(8,128)(2,1)} custom-call(bf16[32,64,640]{2,1,0:T(8,128)(2,1)} %bitcast.10, f32[8,640]{1,0:T(8,128)} %get-tuple-element.13.stat_in, f32[8,640]{1,0:T(8,128)} %get-tuple-element.14.time_ref, bf16[5,640]{1,0:T(8,128)(2,1)} %scale_ref.5, bf16[5,640]{1,0:T(8,128)(2,1)} %shift_ref.5, bf16[4,5760,640]{2,1,0:T(8,128)(2,1)} %bitcast.8), custom_call_target="tpu_custom_call" | custom-call | tf_op jit(solution)/shard_map/res_second/pallas_call | solution.py:700
  205.0 2.6 %copy_out.1 = bf16[4,16,32,640]{3,2,1,0:T(8,128)(2,1)} custom-call(bf16[4,16,32,640]{3,2,1,0:T(8,128)(2,1)} %res_second.1.src_ref), custom_call_target="tpu_custom_call" | custom-call | tf_op jit(solution)/shard_map/copy_out/pallas_call | solution.py:732

commit v9 on v7

--- a/solution.py
+++ b/solution.py
@@ -715,7 +715,7 @@
 
 
 def copy_kernel(src_ref, out_ref, buf_ref, in_sem, out_sem):
-    parts = [(i, slice(j * 8, (j + 1) * 8)) for i in range(src_ref.shape[0]) for j in range(src_ref.shape[1] // 8)]
+    parts = [(i, slice(j * 4, (j + 1) * 4)) for i in range(src_ref.shape[0]) for j in range(src_ref.shape[1] // 4)]
     reads = [pltpu.make_async_copy(src_ref.at[i, rows], buf_ref.at[i, rows], in_sem.at[n]) for n, (i, rows) in enumerate(parts)]
     writes = [pltpu.make_async_copy(buf_ref.at[i, rows], out_ref.at[i, rows], out_sem.at[n]) for n, (i, rows) in enumerate(parts)]
     for read in reads:
@@ -728,7 +728,7 @@
 
 
 def copy_call(src):
-    parts = src.shape[0] * (src.shape[1] // 8)
+    parts = src.shape[0] * (src.shape[1] // 4)
     return pl.pallas_call(
         copy_kernel,
         out_shape=jax.ShapeDtypeStruct(src.shape, src.dtype),

time: 208 us -> 208 us (level)
  no operation moved by 1% of the time
where the time goes in v9:
time: 208 us
  Pallas kernels  208 us (100%)
    pallas_call x1, Pallas kernels, attention_call(): pl.pallas_call(functools.partial(attention_kernel, norm_idx, count, logit...  79.2 us
    pallas_call x1, Pallas kernels, first_call(): pl.pallas_call(functools.partial(first_kernel, count), out_shape=[jax.Sha...  65.5 us
    pallas_call x1, Pallas kernels, second_call(): pl.pallas_call(functools.partial(second_kernel, count), out_shape=jax.Sha...  60.3 us

profile of v9, /device:TPU:1, one launch (start us, length us, event | category | flops | bytes accessed | tf_op | source)
XLA Modules:
  0.0 207.9 jit_solution(14024052651350562462)
XLA Ops:
  0.0 65.5 %res_first.1 = (bf16[32,64,640]{2,1,0:T(8,128)(2,1)}, f32[8,640]{1,0:T(8,128)}, f32[8,640]{1,0:T(8,128)}) custom-call(bf16[4,16,32,640]{3,2,1,0:T(8,128)(2,1)} %x_ref.1, bf16[4,1280]{1,0:T(4,128)(2,1)} %emb_ref.1, bf16[5,640]{1,0:T(8,128)(2,1)} %scale_ref.5, bf16[5,640]{1,0:T(8,128)(2,1)} %shift_ref.5, bf16[4,5760,640]{2,1,0:T(8,128)(2,1)} %bitcast.7, ...), custom_call_target="tpu_custom_call" | custom-call | tf_op jit(solution)/shard_map/res_first/pallas_call | solution.py:672
  65.5 79.2 %attention.1 = (bf16[2048,640]{1,0:T(8,128)(2,1)}, f32[8,640]{1,0:T(8,128)}) custom-call(bf16[2048,640]{1,0:T(8,128)(2,1)} %bitcast.9, f32[8,640]{1,0:T(8,128)} %get-tuple-element.11.stat_in, bf16[5,640]{1,0:T(8,128)(2,1)} %scale_ref.5, bf16[5,640]{1,0:T(8,128)(2,1)} %shift_ref.5, bf16[3,640,640]{2,1,0:T(8,128)(2,1)} %bitcast.11, bf16[640,640]{1,0:T(8,128)(2,1)} %bitcast.12), custom_call_target="tpu_custom_call" | custom-call | tf_op jit(solution)/shard_map/attention/pallas_call | solution.py:746
  144.7 60.3 %res_second.1.src_ref = bf16[4,16,32,640]{3,2,1,0:T(8,128)(2,1)} custom-call(bf16[32,64,640]{2,1,0:T(8,128)(2,1)} %bitcast.10, f32[8,640]{1,0:T(8,128)} %get-tuple-element.13.stat_in, f32[8,640]{1,0:T(8,128)} %get-tuple-element.14.time_ref, bf16[5,640]{1,0:T(8,128)(2,1)} %scale_ref.5, bf16[5,640]{1,0:T(8,128)(2,1)} %shift_ref.5, bf16[4,5760,640]{2,1,0:T(8,128)(2,1)} %bitcast.8), custom_call_target="tpu_custom_call" | custom-call | tf_op jit(solution)/shard_map/res_second/pallas_call | solution.py:700
  205.0 2.8 %copy_out.1 = bf16[4,16,32,640]{3,2,1,0:T(8,128)(2,1)} custom-call(bf16[4,16,32,640]{3,2,1,0:T(8,128)(2,1)} %res_second.1.src_ref), custom_call_target="tpu_custom_call" | custom-call | tf_op jit(solution)/shard_map/copy_out/pallas_call | solution.py:732
